TPU v7x, 8 devices: a whole 2x2x1 slice. The times are simulated.
8 devices in a mesh: dp: 2 (over z, y), tp: 4 (over x, core).
Axes of the slice: x: 2, y: 2, z: 1, core: 2. Of those that a mesh axis runs over, the one named last changes fastest.
Arguments:
- x_in: bfloat16 [1024, 3584], P('dp'), parts along dimension 0
- lengths: int32 [1024], P('dp'), parts along dimension 0
- norm_gain: bfloat16 [2, 3584], replicated
- w_q: bfloat16 [2, 3584, 4096], P(None, None, 'tp')
- w_k: bfloat16 [2, 3584, 2048], P(None, None, 'tp')
- w_v: bfloat16 [2, 3584, 2048], P(None, None, 'tp')
- w_o: bfloat16 [2, 4096, 3584], P(None, 'tp')
- w_gate: bfloat16 [2, 3584, 14336], P(None, None, 'tp')
- w_up: bfloat16 [2, 3584, 14336], P(None, None, 'tp')
- w_down: bfloat16 [2, 14336, 3584], P(None, 'tp')
- k_cache: bfloat16 [2, 1024, 32, 8, 256], P(None, 'dp', None, 'tp'), parts along dimension 1
- v_cache: bfloat16 [2, 1024, 32, 8, 256], P(None, 'dp', None, 'tp'), parts along dimension 1
Outputs:
- output: bfloat16 [1024, 3584], P('dp'), parts along dimension 0
There are 2 independent parts. A program takes and returns all parts, laid end to end along the dimension named above; an argument that names none is the same for every part.
All inputs are finite; a program needn't handle non-finite values.
Results may differ from a plain program's by a relative error of at most 0.0171358.
Values are sent between devices in bfloat16 or wider.
A program may use at most 1.25 GiB of HBM per device.

v0:
```python
import jax
import jax.numpy as jnp
from jax import lax
from jax.sharding import PartitionSpec as P

NORM_EPS = 1e-5
ROPE_BASE = 500000.0


def rms_norm(x_res, gain_row):
    x_f32 = x_res.astype(jnp.float32)
    inv_rms = lax.rsqrt(jnp.mean(x_f32 * x_f32, axis=-1, keepdims=True) + NORM_EPS)
    return (x_f32 * inv_rms * gain_row.astype(jnp.float32)).astype(jnp.bfloat16)


def rope_rotate(head_vecs, positions):
    head_dim = head_vecs.shape[-1]
    half_dim = head_dim // 2
    inv_freq = 1.0 / (ROPE_BASE ** (jnp.arange(0, head_dim, 2).astype(jnp.float32) / head_dim))
    angles = positions.astype(jnp.float32)[:, None] * inv_freq[None, :]
    cos_ang = jnp.cos(angles)[:, None, :]
    sin_ang = jnp.sin(angles)[:, None, :]
    vec_f32 = head_vecs.astype(jnp.float32)
    rot_first = vec_f32[..., :half_dim]
    rot_second = vec_f32[..., half_dim:]
    return jnp.concatenate([rot_first * cos_ang - rot_second * sin_ang, rot_second * cos_ang + rot_first * sin_ang], axis=-1).astype(jnp.bfloat16)


def decode_attention(q_rot, k_rot, v_new, k_layer, v_layer, lengths):
    attn_scale = q_rot.shape[-1] ** -0.5
    seq_len = k_layer.shape[1]
    cache_logits = jnp.einsum('bkgd,bskd->bkgs', q_rot, k_layer, preferred_element_type=jnp.float32) * attn_scale
    valid_mask = jnp.arange(seq_len)[None, :] < lengths[:, None]
    cache_logits = jnp.where(valid_mask[:, None, None, :], cache_logits, -jnp.inf)
    self_logit = jnp.einsum('clhe,cle->clh', q_rot, k_rot, preferred_element_type=jnp.float32) * attn_scale
    row_peak = jnp.maximum(jnp.max(cache_logits, axis=-1), self_logit)
    cache_w = jnp.exp(cache_logits - row_peak[..., None])
    self_w = jnp.exp(self_logit - row_peak)
    prob_denom = jnp.sum(cache_w, axis=-1) + self_w
    cache_p = (cache_w / prob_denom[..., None]).astype(jnp.bfloat16)
    self_p = (self_w / prob_denom).astype(jnp.bfloat16)
    cache_part = jnp.einsum('bkgs,bskd->bkgd', cache_p, v_layer, preferred_element_type=jnp.float32)
    self_part = self_p.astype(jnp.float32)[..., None] * v_new.astype(jnp.float32)[:, :, None, :]
    return (cache_part + self_part).astype(jnp.bfloat16)


def layer_update(x_res, lengths, gain_row, wq_layer, wk_layer, wv_layer, wo_layer, wg_layer, wu_layer, wd_layer, k_layer, v_layer):
    tok_rows = x_res.shape[0]
    head_dim = k_layer.shape[-1]
    kv_local = k_layer.shape[-2]
    normed = rms_norm(x_res, gain_row)
    q_proj = jnp.dot(normed, wq_layer, preferred_element_type=jnp.float32).astype(jnp.bfloat16).reshape(tok_rows, -1, head_dim)
    k_proj = jnp.dot(normed, wk_layer, preferred_element_type=jnp.float32).astype(jnp.bfloat16).reshape(tok_rows, kv_local, head_dim)
    v_new = jnp.dot(normed, wv_layer, preferred_element_type=jnp.float32).astype(jnp.bfloat16).reshape(tok_rows, kv_local, head_dim)
    q_rot = rope_rotate(q_proj, lengths).reshape(tok_rows, kv_local, -1, head_dim)
    k_rot = rope_rotate(k_proj, lengths)
    attn_flat = decode_attention(q_rot, k_rot, v_new, k_layer, v_layer, lengths).reshape(tok_rows, -1)
    gate_act = jnp.dot(normed, wg_layer, preferred_element_type=jnp.float32).astype(jnp.bfloat16)
    up_act = jnp.dot(normed, wu_layer, preferred_element_type=jnp.float32).astype(jnp.bfloat16)
    mlp_hidden = (jax.nn.silu(gate_act.astype(jnp.float32)) * up_act.astype(jnp.float32)).astype(jnp.bfloat16)
    return jnp.dot(attn_flat, wo_layer, preferred_element_type=jnp.float32) + jnp.dot(mlp_hidden, wd_layer, preferred_element_type=jnp.float32)


def solution(mesh):
    tp_size = mesh.shape['tp']
    arg_specs = (P('dp', None), P('dp'), P(), P(None, None, 'tp'), P(None, None, 'tp'), P(None, None, 'tp'), P(None, 'tp', None), P(None, None, 'tp'), P(None, None, 'tp'), P(None, 'tp', None), P(None, 'dp', None, 'tp', None), P(None, 'dp', None, 'tp', None))

    def per_device(x_in, lengths, norm_gain, w_q, w_k, w_v, w_o, w_gate, w_up, w_down, k_cache, v_cache):
        tok_rows, model_width = x_in.shape
        col_width = model_width // tp_size
        col_start = lax.axis_index('tp') * col_width
        x_res = x_in
        for layer_idx in range(norm_gain.shape[0]):
            update = layer_update(x_res, lengths, norm_gain[layer_idx], w_q[layer_idx], w_k[layer_idx], w_v[layer_idx], w_o[layer_idx], w_gate[layer_idx], w_up[layer_idx], w_down[layer_idx], k_cache[layer_idx], v_cache[layer_idx])
            partial_sum = update.astype(jnp.bfloat16)
            received = lax.all_to_all(partial_sum, 'tp', 1, 0, tiled=True)
            reduced = jnp.sum(received.reshape(tp_size, tok_rows, col_width).astype(jnp.float32), axis=0)
            own_cols = lax.dynamic_slice_in_dim(x_res, col_start, col_width, axis=1)
            new_cols = (own_cols.astype(jnp.float32) + reduced).astype(jnp.bfloat16)
            x_res = lax.all_gather(new_cols, 'tp', axis=1, tiled=True)
        return x_res

    return jax.shard_map(per_device, mesh=mesh, in_specs=arg_specs, out_specs=P('dp', None), check_vma=False)
```

profile of v0, /device:TPU:0, one launch (start us, length us, event | category | flops | bytes accessed | tf_op | source)
XLA Modules:
  0.0 544.3 jit_solution(1977534578441696536)
XLA Ops:
  8.1 1.5 convert_reduce_fusion.2
  9.5 2.8 fusion.22
  12.4 5.4 fusion.102
  19.5 1.5 copy.83
  21.0 9.5 %fusion.93 = f32[512,1024]{1,0:T(8,128)} fusion(bf16[2,3584,1024]{2,1,0:T(8,128)(2,1)} %param.15, bf16[512,3584]{1,0:T(8,128)(2,1)} %param.12, f32[3584]{0:T(1024)S(1)} %get-tuple-element.6, f32[512]{0:T(512)S(1)} %add_rsqrt_fusion.1), kind=kOutput, calls=%fused_computation.93 | convolution fusion | flops 3766484992 | bytes 13123584 | tf_op jit(solution)/shard_map/dot_general | solution.py:52
  30.5 2.2 reshape.149
  34.1 2.9 multiply_reduce_fusion.1
  37.2 42.8 %fusion.140 = (bf16[1,512,32,2,256]{4,3,2,1,0:T(2,128)(2,1)}, bf16[1,512,32,2,256]{4,3,2,1,0:T(2,128)(2,1)}) fusion(bf16[2,512,32,2,256]{4,3,2,1,0:T(2,128)(2,1)} %param.22), kind=kLoop, calls=%fused_computation.146 | loop fusion | bytes 67108864 | tf_op jit(solution)/shard_map/slice | solution.py:74
  80.0 8.5 %fusion.142 = (f32[512,2,2]{2,1,0:T(2,128)S(1)}, f32[512,2,2,32]{3,2,1,0:T(2,128)S(1)}) fusion(bf16[1,512,32,2,256]{4,3,2,1,0:T(2,128)(2,1)} %get-tuple-element.8, bf16[512,2,2,128]{3,2,1,0:T(2,128)(2,1)S(1)} %bitcast.159, bf16[512,2,2,128]{3,2,1,0:T(2,128)(2,1)S(1)} %bitcast.157, pred[512,32]{1,0:T(8,128)(4,1)S(1)} %iota_compare_fusion), kind=kOutput, calls=%fused_computation.148 | convolution fusion | flops 35846144 | bytes 18112512 | tf_op jit(solution)/shard_map/bkgd,bskd->bkgs/dot_general | solution.py:32
  89.0 14.5 %fusion.116 = f32[512,2,2]{2,1,0:T(2,128)S(1)} fusion(f32[512,2,2,32]{3,2,1,0:T(2,128)S(1)} %get-tuple-element.26, f32[512,2,2]{2,1,0:T(2,128)S(1)} %copy.51), kind=kLoop, calls=%fused_computation.114 | loop fusion | flops 129024 | bytes 278528 | tf_op jit(solution)/shard_map/reduce_sum | solution.py:39
  103.8 1.0 copy.53
  104.8 1.0 copy.55
  105.8 5.3 fusion.105
  111.6 30.5 %fusion.141 = (bf16[1,512,32,2,256]{4,3,2,1,0:T(2,128)(2,1)S(1)}, bf16[1,512,32,2,256]{4,3,2,1,0:T(2,128)(2,1)}) fusion(bf16[2,512,32,2,256]{4,3,2,1,0:T(2,128)(2,1)} %param.23), kind=kLoop, calls=%fused_computation.147 | loop fusion | bytes 67108864 | tf_op jit(solution)/shard_map/slice | solution.py:74
  142.2 5.7 %add_convert_fusion.3 = bf16[512,2,2,256]{3,2,1,0:T(2,128)(2,1)} fusion(bf16[1,512,32,2,256]{4,3,2,1,0:T(2,128)(2,1)S(1)} %get-tuple-element.9, f32[512,2,256]{2,1,0:T(2,128)S(1)} %copy.56, f32[512,2,2]{2,1,0:T(2,128)S(1)} %copy-done.12, f32[512,2,2,32]{3,2,1,0:T(2,128)S(1)} %get-tuple-element.26, f32[512,2,2]{2,1,0:T(2,128)S(1)} %copy-done.11, ...), kind=kOutput, calls=%fused_computation.89 | convolution fusion | flops 35323904 | bytes 19161088 | tf_op jit(solution)/shard_map/bkgs,bskd->bkgd/dot_general | solution.py:42
  147.8 1.8 reshape.146
  149.6 20.6 %fusion.54 = bf16[512,3584]{1,0:T(8,128)(2,1)} fusion(bf16[2,3584,3584]{2,1,0:T(8,128)(2,1)} %param.19, bf16[512,3584]{1,0:T(8,128)(2,1)} %param.12, f32[3584]{0:T(1024)S(1)} %get-tuple-element.6, f32[512]{0:T(512)S(1)} %add_rsqrt_fusion.1), kind=kOutput, calls=%fused_computation.66 | convolution fusion | flops 13162512384 | bytes 33046528 | tf_op jit(solution)/shard_map/dot_general | solution.py:58
  170.2 9.0 %fusion.40 = f32[512,3584]{1,0:T(8,128)} fusion(bf16[512,1024]{1,0:T(8,128)(2,1)S(1)} %reshape.146, bf16[2,1024,3584]{2,1,0:T(8,128)(2,1)} %param.18), kind=kOutput, calls=%fused_computation.52 | convolution fusion | flops 3758096384 | bytes 15728640 | tf_op jit(solution)/shard_map/dot_general | solution.py:61
  179.3 22.1 %fusion.176 = bf16[512,3584]{1,0:T(8,128)(2,1)} fusion(bf16[512,3584]{1,0:T(8,128)(2,1)} %fusion.54, bf16[2,3584,3584]{2,1,0:T(8,128)(2,1)} %param.20, bf16[512,3584]{1,0:T(8,128)(2,1)} %param.12, f32[3584]{0:T(1024)S(1)} %get-tuple-element.6, f32[512]{0:T(512)S(1)} %add_rsqrt_fusion.1), kind=kOutput, calls=%fused_computation.65.clone.clone.2 | convolution fusion | flops 13177192448 | bytes 36716544 | tf_op jit(solution)/shard_map/dot_general | solution.py:59
  201.4 21.7 %add_convert_fusion.1 = bf16[512,3584]{1,0:T(8,128)(2,1)} fusion(f32[512,3584]{1,0:T(8,128)} %fusion.40, bf16[2,3584,3584]{2,1,0:T(8,128)(2,1)} %param.21, bf16[512,3584]{1,0:T(8,128)(2,1)} %fusion.176), kind=kOutput, calls=%fused_computation.61 | convolution fusion | flops 13157007360 | bytes 40370176 | tf_op jit(solution)/shard_map/dot_general | solution.py:61
  223.0 4.2 copy.116
  227.2 4.7 all-to-all-start
  232.0 43.3 %all-to-all-done = bf16[512,4,896]{2,0,1:T(8,128)(2,1)} async-done(((bf16[512,4,896]{2,0,1:T(8,128)(2,1)}), bf16[512,4,896]{2,0,1:T(8,128)(2,1)}, u32[]{:S(2)}, u32[]{:S(2)}) %all-to-all-start) | async-done | bytes 3670048 | tf_op jit(solution)/shard_map/all_to_all | solution.py:76
  275.3 2.7 convert_reduce_fusion.1
  278.0 2.3 add_convert_fusion.5
  280.4 29.4 %all-gather.3.cloned.1.call-done = bf16[512,3584]{1,0:T(8,128)(2,1)} async-done(((bf16[512,896]{1,0:T(8,128)(2,1)}), bf16[512,3584]{1,0:T(8,128)(2,1)}) %all-gather.3.cloned.1.call-update) | async-done | bytes 3670032 | tf_op jit(solution)/shard_map/all_gather | solution.py:80
  309.8 2.8 fusion.29
  312.6 5.4 fusion.108
  318.5 1.5 copy.84
  320.0 9.6 %fusion.99 = f32[512,1024]{1,0:T(8,128)} fusion(bf16[2,3584,1024]{2,1,0:T(8,128)(2,1)} %param.15, bf16[512,3584]{1,0:T(8,128)(2,1)} %all-gather.3.cloned.1.call-done, f32[3584]{0:T(1024)S(1)} %copy-done.15, f32[512]{0:T(512)S(1)} %add_rsqrt_fusion), kind=kOutput, calls=%fused_computation.95 | convolution fusion | flops 3766484992 | bytes 13123584 | tf_op jit(solution)/shard_map/dot_general | solution.py:52
  329.6 2.2 reshape.153
  333.2 2.9 multiply_reduce_fusion
  336.3 8.7 %fusion.143 = (f32[512,2,2]{2,1,0:T(2,128)S(1)}, f32[512,2,2,32]{3,2,1,0:T(2,128)S(1)}) fusion(bf16[1,512,32,2,256]{4,3,2,1,0:T(2,128)(2,1)} %get-tuple-element.7, bf16[512,2,2,128]{3,2,1,0:T(2,128)(2,1)} %bitcast.155, bf16[512,2,2,128]{3,2,1,0:T(2,128)(2,1)S(1)} %bitcast.153, pred[512,32]{1,0:T(8,128)(4,1)S(1)} %copy-done.14), kind=kOutput, calls=%fused_computation.149 | convolution fusion | flops 35846144 | bytes 18112512 | tf_op jit(solution)/shard_map/bkgd,bskd->bkgs/dot_general | solution.py:32
  345.4 14.5 %fusion.117 = f32[512,2,2]{2,1,0:T(2,128)S(1)} fusion(f32[512,2,2,32]{3,2,1,0:T(2,128)S(1)} %get-tuple-element.28, f32[512,2,2]{2,1,0:T(2,128)S(1)} %copy.60), kind=kLoop, calls=%fused_computation.115 | loop fusion | flops 129024 | bytes 278528 | tf_op jit(solution)/shard_map/reduce_sum | solution.py:39
  360.2 1.0 copy.62
  361.2 1.0 copy.64
  362.3 5.4 fusion.111
  368.1 10.9 %add_convert_fusion.2 = bf16[512,2,2,256]{3,2,1,0:T(2,128)(2,1)} fusion(bf16[1,512,32,2,256]{4,3,2,1,0:T(2,128)(2,1)} %get-tuple-element.10, f32[512,2,256]{2,1,0:T(2,128)S(1)} %copy.65, f32[512,2,2]{2,1,0:T(2,128)} %copy.64, f32[512,2,2,32]{3,2,1,0:T(2,128)S(1)} %get-tuple-element.28, f32[512,2,2]{2,1,0:T(2,128)} %copy.62, f32[512,2,2]{2,1,0:T(2,128)S(1)} %copy.60), kind=kOutput, calls=%fused_computation.88 | convolution fusion | flops 35323904 | bytes 19161088 | tf_op jit(solution)/shard_map/bkgs,bskd->bkgd/dot_general | solution.py:42
  379.0 1.8 reshape.147
  380.8 9.1 %fusion.36 = f32[512,3584]{1,0:T(8,128)} fusion(bf16[512,1024]{1,0:T(8,128)(2,1)S(1)} %reshape.147, bf16[2,1024,3584]{2,1,0:T(8,128)(2,1)} %param.18), kind=kOutput, calls=%fused_computation.48 | convolution fusion | flops 3758096384 | bytes 15728640 | tf_op jit(solution)/shard_map/dot_general | solution.py:61
  389.9 20.9 %fusion.60 = bf16[512,3584]{1,0:T(8,128)(2,1)} fusion(bf16[2,3584,3584]{2,1,0:T(8,128)(2,1)} %param.19, bf16[512,3584]{1,0:T(8,128)(2,1)} %all-gather.3.cloned.1.call-done, f32[3584]{0:T(1024)S(1)} %copy-done.15, f32[512]{0:T(512)S(1)} %add_rsqrt_fusion), kind=kOutput, calls=%fused_computation.68 | convolution fusion | flops 13162512384 | bytes 33046528 | tf_op jit(solution)/shard_map/dot_general | solution.py:58
  410.7 21.7 %fusion.172 = bf16[512,3584]{1,0:T(8,128)(2,1)} fusion(bf16[512,3584]{1,0:T(8,128)(2,1)} %fusion.60, bf16[2,3584,3584]{2,1,0:T(8,128)(2,1)} %param.20, bf16[512,3584]{1,0:T(8,128)(2,1)} %all-gather.3.cloned.1.call-done, f32[3584]{0:T(1024)S(1)} %copy-done.15, f32[512]{0:T(512)S(1)} %add_rsqrt_fusion), kind=kOutput, calls=%fused_computation.64.clone.clone.2 | convolution fusion | flops 13177192448 | bytes 36716544 | tf_op jit(solution)/shard_map/dot_general | solution.py:59
  432.5 21.6 %add_convert_fusion = bf16[512,3584]{1,0:T(8,128)(2,1)} fusion(f32[512,3584]{1,0:T(8,128)} %fusion.36, bf16[2,3584,3584]{2,1,0:T(8,128)(2,1)} %param.21, bf16[512,3584]{1,0:T(8,128)(2,1)} %fusion.172), kind=kOutput, calls=%fused_computation.57 | convolution fusion | flops 13157007360 | bytes 40370176 | tf_op jit(solution)/shard_map/dot_general | solution.py:61
  454.1 2.3 copy.115
  456.4 45.1 %all_to_all.26 = bf16[512,4,896]{2,0,1:T(8,128)(2,1)S(1)} all-to-all(bf16[512,4,896]{2,0,1:T(8,128)(2,1)S(1)} %bitcast.149), channel_id=1, replica_groups=mesh['dp'=2,'tp'=4] {'tp'}, dimensions={1} | all-to-all | bytes 7340032 | tf_op jit(solution)/shard_map/all_to_all | solution.py:76
  502.0 2.3 add_convert_fusion.4
  504.3 28.6 %all-gather.5.cloned.1.call-done = bf16[512,3584]{1,0:T(8,128)(2,1)} async-done(((bf16[512,896]{1,0:T(8,128)(2,1)}), bf16[512,3584]{1,0:T(8,128)(2,1)}) %all-gather.5.cloned.1.call-update) | async-done | bytes 3670032 | tf_op jit(solution)/shard_map/all_gather | solution.py:80
  532.9 4.1 copy.118
  (67 shorter events, 9.7 us)
Async XLA Ops:
  8.1 72.0 %copy-start.13 = (pred[512,32]{1,0:T(8,128)(4,1)}, pred[512,32]{1,0:T(8,128)(4,1)S(1)}, u32[]{:S(2)}) copy-start(pred[512,32]{1,0:T(8,128)(4,1)S(1)} %iota_compare_fusion) | copy-start | bytes 49156
  18.8 13.9 %copy-start = (f32[512,128]{1,0:T(8,128)}, f32[512,128]{1,0:T(8,128)S(1)}, u32[]{:S(2)}) copy-start(f32[512,128]{1,0:T(8,128)S(1)} %get-tuple-element.23) | copy-start | bytes 786436
  18.9 13.9 %copy-start.2 = (f32[512,128]{1,0:T(8,128)}, f32[512,128]{1,0:T(8,128)S(1)}, u32[]{:S(2)}) copy-start(f32[512,128]{1,0:T(8,128)S(1)} %get-tuple-element.24) | copy-start | bytes 786436
  19.0 2.0 copy-start.4
  19.1 1.9 copy-start.6
  33.3 0.8 copy-start.9
  37.2 42.8 %copy-start.10 = (bf16[512,4,128]{2,1,0:T(4,128)(2,1)S(1)}, bf16[512,4,128]{2,1,0:T(4,128)(2,1)}, u32[]{:S(2)}) copy-start(bf16[512,4,128]{2,1,0:T(4,128)(2,1)} %copy-done.9) | copy-start | bytes 1572868
  111.6 30.5 %copy-start.11 = (f32[512,2,2]{2,1,0:T(2,128)S(1)}, f32[512,2,2]{2,1,0:T(2,128)}, u32[]{:S(2)}) copy-start(f32[512,2,2]{2,1,0:T(2,128)} %copy.53) | copy-start | bytes 24580
  111.6 30.5 %copy-start.12 = (f32[512,2,2]{2,1,0:T(2,128)S(1)}, f32[512,2,2]{2,1,0:T(2,128)}, u32[]{:S(2)}) copy-start(f32[512,2,2]{2,1,0:T(2,128)} %copy.55) | copy-start | bytes 24580
  227.2 48.1 %all-to-all-start = ((bf16[512,4,896]{2,0,1:T(8,128)(2,1)}), bf16[512,4,896]{2,0,1:T(8,128)(2,1)}, u32[]{:S(2)}, u32[]{:S(2)}) async-start(bf16[512,4,896]{2,0,1:T(8,128)(2,1)} %bitcast.148), calls=%async_computation | async-start | bytes 7340032 | tf_op jit(solution)/shard_map/all_to_all | solution.py:76
  232.0 80.7 %copy-start.15 = (f32[3584]{0:T(1024)S(1)}, f32[3584]{0:T(1024)}, u32[]{:S(2)}) copy-start(f32[3584]{0:T(1024)} %get-tuple-element.5) | copy-start | bytes 43012
  232.0 77.8 %all-gather.3.cloned.1.call-start = ((), (), s32[]{:S(2)}) async-start(), calls=%async_computation.2 | async-start | bytes 4587520 | tf_op jit(solution)/shard_map/all_gather | solution.py:80
  280.3 252.6 %all-gather.5.cloned.1.call-start = ((), (), s32[]{:S(2)}) async-start(), calls=%async_computation.3 | async-start | bytes 4587520 | tf_op jit(solution)/shard_map/all_gather | solution.py:80
  312.6 5.6 %copy-start.5 = (f32[512,128]{0,1:T(8,128)S(1)}, f32[512,128]{0,1:T(8,128)}, u32[]{:S(2)}) copy-start(f32[512,128]{0,1:T(8,128)} %copy-done.4) | copy-start | bytes 786436
  312.6 5.6 %copy-start.7 = (f32[512,128]{0,1:T(8,128)S(1)}, f32[512,128]{0,1:T(8,128)}, u32[]{:S(2)}) copy-start(f32[512,128]{0,1:T(8,128)} %copy-done.6) | copy-start | bytes 786436
  320.0 11.8 %copy-start.1 = (f32[512,128]{1,0:T(8,128)S(1)}, f32[512,128]{1,0:T(8,128)}, u32[]{:S(2)}) copy-start(f32[512,128]{1,0:T(8,128)} %copy-done) | copy-start | bytes 786436
  320.0 11.8 %copy-start.3 = (f32[512,128]{1,0:T(8,128)S(1)}, f32[512,128]{1,0:T(8,128)}, u32[]{:S(2)}) copy-start(f32[512,128]{1,0:T(8,128)} %copy-done.2) | copy-start | bytes 786436
  329.6 6.7 %copy-start.14 = (pred[512,32]{1,0:T(8,128)(4,1)S(1)}, pred[512,32]{1,0:T(8,128)(4,1)}, u32[]{:S(2)}) copy-start(pred[512,32]{1,0:T(8,128)(4,1)} %copy-done.13) | copy-start | bytes 49156
  332.4 0.8 copy-start.8
Sparse Core Ops, SparseCore 0:
  280.4 29.2 all-gather.2
  504.4 28.4 all-gather.4
where the time goes:
time: 549 us; the launch traced here: 544 us
  matrix products  221 us (40%)
  local copies, waits for them, and re-layouts  104 us (19%)
  waiting for transfers between devices  101 us (18%)
  other arithmetic  54.3 us (10%)
  blocking collectives  45.1 us (8%)
  between operations  14.3 us (3%)
    all_gather x2, waiting for transfers between devices, per_device(): x_res = lax.all_gather(new_cols, 'tp', axis=1, tiled=True)  58 us
    all_to_all x1, blocking collectives, per_device(): received = lax.all_to_all(partial_sum, 'tp', 1, 0, tiled=True)  45.1 us
    dot_general x2, matrix products, layer_update(): jnp.dot(normed, wu_layer, preferred_element_type=jnp.float32)  43.8 us
    dot_general x2, matrix products, layer_update(): jnp.dot(mlp_hidden, wd_layer, preferred_element_type=jnp.float32)  43.3 us
    all_to_all x1, waiting for transfers between devices, per_device(): received = lax.all_to_all(partial_sum, 'tp', 1, 0, tiled=True)  43.3 us
    slice x1, local copies, waits for them, and re-layouts, per_device(): k_cache[layer_idx]  42.8 us
    dot_general x2, matrix products, layer_update(): jnp.dot(normed, wg_layer, preferred_element_type=jnp.float32)  41.5 us
    slice x1, local copies, waits for them, and re-layouts, per_device(): v_cache[layer_idx]  30.5 us
  transfers between devices with their start and end apart: 3, of which 3 were waited for; matrix products, arithmetic and copies ran while one was open for 0% of the time, Pallas kernels for 0%

commit v1 on v0

v1 whole, which is shorter than its diff:
```python
import functools

import jax
import jax.numpy as jnp
from jax import lax
from jax.experimental import pallas as pl
from jax.experimental.pallas import tpu as pltpu
from jax.sharding import PartitionSpec as P

NORM_EPS = 1e-5
ROPE_BASE = 500000.0
MESH = pl.DeviceIdType.MESH

ROWS = 256
HALF = 128
TILE = 512
SLOTS = 7
WO_SLOTS = 2
KV_SLOTS = 4
KV_TOK = 16


def kernel(cfg, lens_ref, cos_ref, sin_ref, gain_ref, x_in, wq, wk, wv, wo, wg, wu, wd, kc, vc, x_out,
           xs, a_s, q_s, k_s, v_s, att_s, u_s, graw, uraw, sidx, wbuf, wobuf, kbuf, vbuf, ybuf, irecv, rown, xrecv,
           wsem, wosem, kvsem, xsem, isend, irsem, xsend, xrsem, nsend, nrsem, osem):
    layers, tokens, width, seq, kv_heads = cfg
    tok_rows = seq * kv_heads * 2
    chunks = tokens // ROWS
    stages = layers * chunks
    n_dn = width // TILE
    n_ff = wg.shape[2] // TILE
    n_q = wq.shape[2] // TILE
    n_w = n_q + 2 + 2 * n_ff + n_dn
    n_kv = ROWS // KV_TOK
    all_w, all_wo, all_kv = stages * n_w, stages * n_dn, stages * n_kv

    tp = lax.axis_index("tp")
    core = lax.rem(tp, 2)
    sib = tp + 1 - 2 * core
    partner = lax.rem(tp + 2, 4)
    own_row = pl.multiple_of(core * HALF, HALF)
    sib_row = pl.multiple_of((1 - core) * HALF, HALF)

    def w_start(gt):
        st = lax.div(gt, n_w)
        t = gt - st * n_w
        layer = lax.div(st, chunks)
        slot = lax.rem(gt, SLOTS)

        def put(src):
            pltpu.make_async_copy(src, wbuf.at[slot], wsem.at[slot]).start()

        def cols(i):
            return pl.ds(pl.multiple_of(i * TILE, TILE), TILE)

        f = t - (n_q + 2)

        @pl.when(t < n_q)
        def _():
            put(wq.at[layer, :, cols(t)])

        @pl.when(t == n_q)
        def _():
            put(wk.at[layer])

        @pl.when(t == n_q + 1)
        def _():
            put(wv.at[layer])

        @pl.when((f >= 0) & (f < 2 * n_ff) & (lax.rem(f + 2, 2) == 0))
        def _():
            put(wg.at[layer, :, cols(lax.div(f, 2))])

        @pl.when((f >= 0) & (f < 2 * n_ff) & (lax.rem(f + 2, 2) == 1))
        def _():
            put(wu.at[layer, :, cols(lax.div(f, 2))])

        @pl.when(f >= 2 * n_ff)
        def _():
            put(wd.at[layer, :, cols(f - 2 * n_ff)])

    def w_next(gt):
        @pl.when(gt + SLOTS < all_w)
        def _():
            w_start(gt + SLOTS)

    def w_wait(gt):
        slot = lax.rem(gt, SLOTS)
        pltpu.make_async_copy(wk.at[0], wbuf.at[slot], wsem.at[slot]).wait()
        return slot

    def wo_copy(go):
        st = lax.div(go, n_dn)
        j = go - st * n_dn
        slot = lax.rem(go, WO_SLOTS)
        cols = pl.ds(pl.multiple_of(j * TILE, TILE), TILE)
        return pltpu.make_async_copy(wo.at[lax.div(st, chunks), :, cols], wobuf.at[slot], wosem.at[slot])

    def kv_copies(gb):
        st = lax.div(gb, n_kv)
        b = gb - st * n_kv
        layer = lax.div(st, chunks)
        tok = layer * tokens + (st - layer * chunks) * ROWS + b * KV_TOK
        slot = lax.rem(gb, KV_SLOTS)
        rows = pl.ds(pl.multiple_of(tok * tok_rows, KV_TOK * tok_rows), KV_TOK * tok_rows)
        return (pltpu.make_async_copy(kc.at[rows], kbuf.at[slot], kvsem.at[0, slot]),
                pltpu.make_async_copy(vc.at[rows], vbuf.at[slot], kvsem.at[1, slot]))

    def chip_copy(par, j):
        return pltpu.make_async_remote_copy(
            src_ref=ybuf.at[j, pl.ds(sib_row, HALF)], dst_ref=irecv.at[par, j], send_sem=isend.at[j],
            recv_sem=irsem.at[par, j], device_id={"tp": sib}, device_id_type=MESH)

    def link_copy(par, j):
        return pltpu.make_async_remote_copy(
            src_ref=rown.at[j], dst_ref=xrecv.at[par, j], send_sem=xsend.at[j],
            recv_sem=xrsem.at[par, j], device_id={"tp": partner}, device_id_type=MESH)

    def x_piece(par, row, j):
        return xs.at[pl.ds(pl.multiple_of(par * ROWS + row, HALF), HALF), pl.ds(pl.multiple_of(j * TILE, TILE), TILE)]

    def new_copy(par, j):
        piece = x_piece(par, own_row, j)
        return pltpu.make_async_remote_copy(
            src_ref=piece, dst_ref=piece, send_sem=nsend.at[par, j],
            recv_sem=nrsem.at[par, j], device_id={"tp": sib}, device_id_type=MESH)

    def chip_sum(par, j):
        chip_copy(par, j).wait_recv()
        rown[j] = (ybuf[j, pl.ds(own_row, HALF)] + irecv[par, j]).astype(jnp.bfloat16)
        link_copy(par, j).start()

    def finish(par):
        def step(j, _):
            link_copy(par, j).wait()
            chip_copy(par, j).wait_send()
            piece = x_piece(par, own_row, j)
            total = rown[j].astype(jnp.float32) + xrecv[par, j].astype(jnp.float32)
            piece[...] = (piece[...].astype(jnp.float32) + total).astype(jnp.bfloat16)
            new_copy(par, j).start()
            return 0

        lax.fori_loop(0, n_dn, step, 0)

    def new_wait(par):
        def step(j, _):
            new_copy(par, j).wait()
            return 0

        lax.fori_loop(0, n_dn, step, 0)

    def x_copy(c):
        rows = pl.ds(pl.multiple_of(c * ROWS, ROWS), ROWS)
        return pltpu.make_async_copy(x_in.at[rows], xs.at[rows], xsem.at[c])

    def out_copy(c):
        rows = pl.ds(c * ROWS, ROWS)
        return pltpu.make_async_copy(xs.at[rows], x_out.at[rows], osem.at[c])

    for c in range(chunks):
        x_copy(c).start()
    for g in range(SLOTS):
        w_start(jnp.int32(g))
    for g in range(KV_SLOTS):
        for cp in kv_copies(jnp.int32(g)):
            cp.start()
    for g in range(WO_SLOTS):
        wo_copy(jnp.int32(g)).start()

    barrier = pltpu.get_barrier_semaphore()
    for other in (sib, partner):
        pl.semaphore_signal(barrier, inc=1, device_id={"tp": other}, device_id_type=MESH)
    pl.semaphore_wait(barrier, 2)

    n_key = 8 * tok_rows
    lane = lax.broadcasted_iota(jnp.int32, (32, n_key), 1)
    row = lax.broadcasted_iota(jnp.int32, (32, n_key), 0)
    per = 2 * kv_heads
    match = (lax.div(lane, tok_rows) == lax.rem(row, 8)) & (lax.rem(lane, kv_heads) == lax.div(row, 16)) & (lax.rem(lane, per) < kv_heads)
    sidx[...] = jnp.where(match, lax.rem(lax.div(lane, per), seq), 2 * seq)

    def rope(y, base, dst, col, rows):
        cos, sin = cos_ref[rows], sin_ref[rows]
        for h in range(TILE // 256):
            first = y[:, h * 256:h * 256 + 128].astype(jnp.bfloat16).astype(jnp.float32)
            second = y[:, h * 256 + 128:h * 256 + 256].astype(jnp.bfloat16).astype(jnp.float32)
            at = col + h * 256
            dst[:, at:at + 128] = (first * cos - second * sin).astype(jnp.bfloat16).astype(jnp.float32)
            dst[:, at + 128:at + 256] = (second * cos + first * sin).astype(jnp.bfloat16).astype(jnp.float32)

    def dot(a, b):
        return jnp.dot(a, b, preferred_element_type=jnp.float32)

    def attend(slot, b, c, half):
        base = pl.multiple_of(b * KV_TOK, KV_TOK) + half * 8
        base = pl.multiple_of(base, 8)
        tok = pl.ds(base, 8)
        q8, k8, v8 = q_s[tok], k_s[tok], v_s[tok]
        q = jnp.concatenate([q8[:, h * 256:(h + 1) * 256] for h in range(4)], 0)
        kn = jnp.concatenate([k8[:, (h // 2) * 256:(h // 2 + 1) * 256] for h in range(4)], 0)
        vn = jnp.concatenate([v8[:, (h // 2) * 256:(h // 2 + 1) * 256] for h in range(4)], 0)
        len8 = lens_ref[pl.ds(pl.multiple_of(c * ROWS + base, 8), 8), :]
        lens = jnp.concatenate([len8] * 4, 0)
        scale = 1.0 / 16.0
        qq = jnp.concatenate([q[:, :128], q[:, 128:]], 0).astype(jnp.bfloat16)
        rows = pl.ds(half * 8 * tok_rows, 8 * tok_rows)
        s2 = lax.dot_general(qq, kbuf[slot, rows], (((1,), (1,)), ((), ())), preferred_element_type=jnp.float32)
        s = (s2[:32] + jnp.concatenate([s2[32:, 2:], s2[32:, :2]], 1)) * scale
        s = jnp.where(sidx[...] < lens, s, -jnp.inf)
        self_logit = jnp.sum(q * kn, axis=-1, keepdims=True) * scale
        peak = jnp.maximum(jnp.max(s, axis=-1, keepdims=True), self_logit)
        w = jnp.exp(s - peak)
        sw = jnp.exp(self_logit - peak)
        inv = 1.0 / (jnp.sum(w, axis=-1, keepdims=True) + sw)
        p = w * inv
        sp = (sw * inv).astype(jnp.bfloat16).astype(jnp.float32)
        pp = jnp.concatenate([p, jnp.concatenate([p[:, n_key - 2:], p[:, :n_key - 2]], 1)], 0).astype(jnp.bfloat16)
        o2 = dot(pp, vbuf[slot, rows])
        return jnp.concatenate([o2[:32], o2[32:]], 1) + sp * vn

    def swiglu(i):
        g = graw[...].astype(jnp.float32)
        u = uraw[...].astype(jnp.float32)
        u_s[:, pl.ds(pl.multiple_of(i * TILE, TILE), TILE)] = (g * (1.0 / (1.0 + jnp.exp(-g))) * u).astype(jnp.bfloat16)

    def stage(st, _):
        layer = lax.div(st, chunks)
        c = st - layer * chunks
        par = c
        rows = pl.ds(pl.multiple_of(c * ROWS, ROWS), ROWS)
        w0 = st * n_w

        @pl.when(st < chunks)
        def _():
            x_copy(c).wait()

        @pl.when(st >= chunks)
        def _():
            new_wait(par)

        gains = gain_ref[...].astype(jnp.float32)
        gain = gains[:1]
        for other in range(1, layers):
            gain = jnp.where(layer == other, gains[other:other + 1], gain)

        def norm(i, _):
            r = pl.ds(pl.multiple_of(c * ROWS + i * 32, 32), 32)
            x = xs[r].astype(jnp.float32)
            inv = lax.rsqrt(jnp.sum(x * x, axis=-1, keepdims=True) / width + NORM_EPS)
            a_s[pl.ds(pl.multiple_of(i * 32, 32), 32)] = (x * inv * gain).astype(jnp.bfloat16)
            return 0

        lax.fori_loop(0, ROWS // 32, norm, 0)

        @pl.when(st >= 1)
        def _():
            for j in range(n_dn - 2, n_dn):
                chip_sum(1 - par, j)

        s0, s1 = w_wait(w0), w_wait(w0 + 1)
        rope(dot(a_s[...], wbuf[s0]), 0, q_s, 0, rows)
        rope(dot(a_s[...], wbuf[s1]), 0, q_s, TILE, rows)
        w_next(w0)
        w_next(w0 + 1)
        s0, s1 = w_wait(w0 + 2), w_wait(w0 + 3)
        rope(dot(a_s[...], wbuf[s0]), 0, k_s, 0, rows)
        v_s[...] = dot(a_s[...], wbuf[s1]).astype(jnp.bfloat16).astype(jnp.float32)
        w_next(w0 + 2)
        w_next(w0 + 3)

        def block(b, _):
            gb = st * n_kv + b
            slot = lax.rem(gb, KV_SLOTS)
            for cp in kv_copies(gb):
                cp.wait()
            o0, o1 = attend(slot, b, c, 0), attend(slot, b, c, 1)
            t = pl.ds(pl.multiple_of(b * KV_TOK, KV_TOK), KV_TOK)
            for h in range(4):
                o = jnp.concatenate([o0[h * 8:h * 8 + 8], o1[h * 8:h * 8 + 8]], 0)
                att_s[t, h * 256:(h + 1) * 256] = o.astype(jnp.bfloat16)

            @pl.when(gb + KV_SLOTS < all_kv)
            def _():
                for cp in kv_copies(gb + KV_SLOTS):
                    cp.start()

            return 0

        lax.fori_loop(0, n_kv, block, 0)

        def ff(i, _):
            gt = w0 + n_q + 2 + 2 * i
            s0, s1 = w_wait(gt), w_wait(gt + 1)
            swiglu(lax.rem(i + n_ff - 1, n_ff))
            graw[...] = dot(a_s[...], wbuf[s0]).astype(jnp.bfloat16)
            uraw[...] = dot(a_s[...], wbuf[s1]).astype(jnp.bfloat16)
            w_next(gt)
            w_next(gt + 1)
            return 0

        lax.fori_loop(0, n_ff, ff, 0)
        swiglu(n_ff - 1)

        @pl.when(st >= 1)
        def _():
            finish(1 - par)

        def down(j, _):
            gt = w0 + n_q + 2 + 2 * n_ff + j
            go = st * n_dn + j
            s0 = w_wait(gt)
            wo_copy(go).wait()

            @pl.when(j >= 2)
            def _():
                chip_sum(par, j - 2)

            ybuf[j] = dot(u_s[...], wbuf[s0]) + dot(att_s[...], wobuf[lax.rem(go, WO_SLOTS)])
            chip_copy(par, j).start()
            w_next(gt)

            @pl.when(go + WO_SLOTS < all_wo)
            def _():
                wo_copy(go + WO_SLOTS).start()

            return 0

        lax.fori_loop(0, n_dn, down, 0)
        return 0

    graw[...] = jnp.zeros_like(graw)
    uraw[...] = jnp.zeros_like(uraw)
    lax.fori_loop(0, stages, stage, 0)

    last = (stages - 1) % chunks
    for j in range(n_dn - 2, n_dn):
        chip_sum(last, j)
    new_wait(1 - last)
    out_copy(1 - last).start()
    finish(last)
    new_wait(last)
    out_copy(last).start()
    for c in range(chunks):
        out_copy(c).wait()


def solution(mesh):
    arg_specs = (P('dp', None), P('dp'), P(), P(None, None, 'tp'), P(None, None, 'tp'), P(None, None, 'tp'), P(None, 'tp', None), P(None, None, 'tp'), P(None, None, 'tp'), P(None, 'tp', None), P(None, 'dp', None, 'tp', None), P(None, 'dp', None, 'tp', None))

    def per_device(x_in, lengths, norm_gain, w_q, w_k, w_v, w_o, w_gate, w_up, w_down, k_cache, v_cache):
        layers, tokens, seq, kv_heads, head = k_cache.shape
        width = x_in.shape[1]
        half = head // 2
        inv_freq = 1.0 / (ROPE_BASE ** (jnp.arange(0, head, 2).astype(jnp.float32) / head))
        angles = lengths.astype(jnp.float32)[:, None] * inv_freq[None, :]
        cos, sin = jnp.cos(angles), jnp.sin(angles)

        def rows_of(cache):
            r = cache.reshape(layers * tokens * seq, kv_heads, 2, half).transpose(0, 2, 1, 3)
            return r.reshape(layers * tokens * seq * kv_heads * 2, half)

        tok_rows = seq * kv_heads * 2
        n_dn = width // TILE
        vm = pl.BlockSpec(memory_space=pltpu.VMEM)
        hbm = pl.BlockSpec(memory_space=pl.ANY)
        bf, f32 = jnp.bfloat16, jnp.float32
        dma = pltpu.SemaphoreType.DMA
        return pl.pallas_call(
            functools.partial(kernel, (layers, tokens, width, seq, kv_heads)),
            out_shape=jax.ShapeDtypeStruct(x_in.shape, bf),
            in_specs=[vm] * 4 + [hbm] * 10,
            out_specs=hbm,
            scratch_shapes=[
                pltpu.VMEM((tokens, width), bf),
                pltpu.VMEM((ROWS, width), bf),
                pltpu.VMEM((ROWS, w_q.shape[2]), f32),
                pltpu.VMEM((ROWS, w_k.shape[2]), f32),
                pltpu.VMEM((ROWS, w_v.shape[2]), f32),
                pltpu.VMEM((ROWS, w_q.shape[2]), bf),
                pltpu.VMEM((ROWS, w_gate.shape[2]), bf),
                pltpu.VMEM((ROWS, TILE), bf),
                pltpu.VMEM((ROWS, TILE), bf),
                pltpu.VMEM((32, 8 * tok_rows), jnp.int32),
                pltpu.VMEM((SLOTS, width, TILE), bf),
                pltpu.VMEM((WO_SLOTS, w_o.shape[1], TILE), bf),
                pltpu.VMEM((KV_SLOTS, KV_TOK * tok_rows, half), bf),
                pltpu.VMEM((KV_SLOTS, KV_TOK * tok_rows, half), bf),
                pltpu.VMEM((n_dn, ROWS, TILE), f32),
                pltpu.VMEM((2, n_dn, HALF, TILE), f32),
                pltpu.VMEM((n_dn, HALF, TILE), bf),
                pltpu.VMEM((2, n_dn, HALF, TILE), bf),
                dma((SLOTS,)), dma((WO_SLOTS,)), dma((2, KV_SLOTS)), dma((2,)),
                dma((n_dn,)), dma((2, n_dn)), dma((n_dn,)), dma((2, n_dn)), dma((2, n_dn)), dma((2, n_dn)), dma((2,)),
            ],
            compiler_params=pltpu.CompilerParams(
                collective_id=0, has_side_effects=True, vmem_limit_bytes=67_043_328),
            name="decoder",
        )(lengths[:, None], cos, sin, norm_gain, x_in, w_q, w_k, w_v, w_o, w_gate, w_up, w_down,
          rows_of(k_cache), rows_of(v_cache))

    return jax.shard_map(per_device, mesh=mesh, in_specs=arg_specs, out_specs=P('dp', None), check_vma=False)
```

time: 549 us -> 250 us (0.46)
  Pallas kernels: 0 us -> 242 us
  matrix products: 221 us -> 0 us
  waiting for transfers between devices: 101 us -> 0 us
  local copies, waits for them, and re-layouts: 104 us -> 5.64 us
  other arithmetic: 54.3 us -> 2.51 us
  blocking collectives: 45.1 us -> 0 us
  between operations: 14.3 us -> 0.01 us
    pallas_call x0 -> x1, Pallas kernels: none -> 242 us  [per_device(): pl.pallas_call(functools.partial(kernel, (layers, tokens, width, seq, kv_...]
    dot_general x18 -> x0, matrix products: 221 us -> none  [the longest x2 43.8 us: layer_update(): jnp.dot(normed, wu_layer, preferred_element_type=jnp.float32)]
    slice x2 -> x0, local copies, waits for them, and re-layouts: 73.3 us -> none  [the longest x1 42.8 us: per_device(): k_cache[layer_idx]]
    all_gather x2 -> x0, waiting for transfers between devices: 58 us -> none  [per_device(): x_res = lax.all_gather(new_cols, 'tp', axis=1, tiled=True)]
    all_to_all x1 -> x0, blocking collectives: 45.1 us -> none  [per_device(): received = lax.all_to_all(partial_sum, 'tp', 1, 0, tiled=True)]
    all_to_all x1 -> x0, waiting for transfers between devices: 43.3 us -> none  [per_device(): received = lax.all_to_all(partial_sum, 'tp', 1, 0, tiled=True)]
    reduce_sum x6 -> x0, other arithmetic: 37.9 us -> none  [the longest x2 29 us: decode_attention(): prob_denom = jnp.sum(cache_w, axis=-1) + self_w]
    convert_element_type x6 -> x0, local copies, waits for them, and re-layouts: 7.35 us -> none  [the longest x2 4.43 us: rope_rotate(): vec_f32 = head_vecs.astype(jnp.float32)]
  transfers between devices with their start and end apart: 3 -> 0, of which waited for: 3 -> 0; matrix products, arithmetic and copies ran while one was open for 0% -> 0% of each run, Pallas kernels for 0% -> 0%
where the time goes in v1:
time: 250 us
  Pallas kernels  242 us (97%)
  local copies, waits for them, and re-layouts  5.64 us (2%)
  other arithmetic  2.51 us (1%)
    pallas_call x1, Pallas kernels, per_device(): pl.pallas_call(functools.partial(kernel, (layers, tokens, width, seq, kv_...  242 us

profile of v1, /device:TPU:0, one launch (start us, length us, event | category | flops | bytes accessed | tf_op | source)
XLA Modules:
  0.0 249.7 jit_solution(14213420729006135305)
XLA Ops:
  0.0 0.7 convert_element_type.10
  0.7 1.5 copy.17.lens_ref
  2.2 1.8 multiply_sine_fusion
  4.0 241.5 %decoder.1 = bf16[512,3584]{1,0:T(8,128)(2,1)} custom-call(s32[512,1]{1,0:T(8,128)} %copy.17.lens_ref, f32[512,128]{1,0:T(8,128)} %get-tuple-element.6.cos_ref, f32[512,128]{1,0:T(8,128)} %get-tuple-element.5.sin_ref, bf16[2,3584]{1,0:T(2,128)(2,1)} %gain_ref.1, bf16[512,3584]{1,0:T(8,128)(2,1)} %x_in.1, bf16[2,3584,1024]{2,1,0:T(8,128)(2,1)} %wq.1, ...), custom_call_target="tpu_custom_call" | custom-call | tf_op jit(solution)/shard_map/decoder/pallas_call | solution.py:368
  245.6 4.1 %copy.19 = bf16[512,3584]{1,0:T(8,128)(2,1)} copy(bf16[512,3584]{1,0:T(8,128)(2,1)} %decoder.1) | data formatting | bytes 7340032
  (1 shorter events, 0.0 us)

commit v2 on v1

--- a/solution.py
+++ b/solution.py
@@ -15,9 +15,8 @@
 HALF = 128
 TILE = 512
 SLOTS = 7
-WO_SLOTS = 2
-KV_SLOTS = 4
-KV_TOK = 16
+KV_SLOTS = 3
+KV_TOK = 32
 
 
 def kernel(cfg, lens_ref, cos_ref, sin_ref, gain_ref, x_in, wq, wk, wv, wo, wg, wu, wd, kc, vc, x_out,
@@ -32,7 +31,7 @@
     n_q = wq.shape[2] // TILE
     n_w = n_q + 2 + 2 * n_ff + n_dn
     n_kv = ROWS // KV_TOK
-    all_w, all_wo, all_kv = stages * n_w, stages * n_dn, stages * n_kv
+    all_w, all_kv = stages * n_w, stages * n_kv
 
     tp = lax.axis_index("tp")
     core = lax.rem(tp, 2)
@@ -89,12 +88,9 @@
         pltpu.make_async_copy(wk.at[0], wbuf.at[slot], wsem.at[slot]).wait()
         return slot
 
-    def wo_copy(go):
-        st = lax.div(go, n_dn)
-        j = go - st * n_dn
-        slot = lax.rem(go, WO_SLOTS)
+    def wo_copy(layer, j):
         cols = pl.ds(pl.multiple_of(j * TILE, TILE), TILE)
-        return pltpu.make_async_copy(wo.at[lax.div(st, chunks), :, cols], wobuf.at[slot], wosem.at[slot])
+        return pltpu.make_async_copy(wo.at[layer, :, cols], wobuf.at[j], wosem.at[j])
 
     def kv_copies(gb):
         st = lax.div(gb, n_kv)
@@ -164,8 +160,8 @@
     for g in range(KV_SLOTS):
         for cp in kv_copies(jnp.int32(g)):
             cp.start()
-    for g in range(WO_SLOTS):
-        wo_copy(jnp.int32(g)).start()
+    for j in range(n_dn):
+        wo_copy(0, j).start()
 
     barrier = pltpu.get_barrier_semaphore()
     for other in (sib, partner):
@@ -191,31 +187,35 @@
     def dot(a, b):
         return jnp.dot(a, b, preferred_element_type=jnp.float32)
 
-    def attend(slot, b, c, half):
-        base = pl.multiple_of(b * KV_TOK, KV_TOK) + half * 8
-        base = pl.multiple_of(base, 8)
-        tok = pl.ds(base, 8)
-        q8, k8, v8 = q_s[tok], k_s[tok], v_s[tok]
-        q = jnp.concatenate([q8[:, h * 256:(h + 1) * 256] for h in range(4)], 0)
+    scale = 1.0 / 16.0
+
+    def roll(x, by):
+        return jnp.concatenate([pltpu.roll(x[:, i:i + 128], by % 128, axis=1) for i in range(0, n_key, 128)], 1)
+
+    def logits(slot, b, c, part):
+        base = pl.multiple_of(b * KV_TOK + part * 8, 8)
+        q8, k8 = q_s[pl.ds(base, 8)], k_s[pl.ds(base, 8)]
+        q = jnp.concatenate([q8[:, h * 256:(h + 1) * 256] for h in range(4)], 0) * scale
         kn = jnp.concatenate([k8[:, (h // 2) * 256:(h // 2 + 1) * 256] for h in range(4)], 0)
-        vn = jnp.concatenate([v8[:, (h // 2) * 256:(h // 2 + 1) * 256] for h in range(4)], 0)
         len8 = lens_ref[pl.ds(pl.multiple_of(c * ROWS + base, 8), 8), :]
         lens = jnp.concatenate([len8] * 4, 0)
-        scale = 1.0 / 16.0
         qq = jnp.concatenate([q[:, :128], q[:, 128:]], 0).astype(jnp.bfloat16)
-        rows = pl.ds(half * 8 * tok_rows, 8 * tok_rows)
-        s2 = lax.dot_general(qq, kbuf[slot, rows], (((1,), (1,)), ((), ())), preferred_element_type=jnp.float32)
-        s = (s2[:32] + jnp.concatenate([s2[32:, 2:], s2[32:, :2]], 1)) * scale
-        s = jnp.where(sidx[...] < lens, s, -jnp.inf)
-        self_logit = jnp.sum(q * kn, axis=-1, keepdims=True) * scale
+        keys = kbuf[slot, pl.ds(part * n_key, n_key)]
+        s2 = lax.dot_general(qq, keys, (((1,), (1,)), ((), ())), preferred_element_type=jnp.float32)
+        s = s2[:32] + roll(s2[32:], -2)
+        return jnp.where(sidx[...] < lens, s, -jnp.inf), jnp.sum(q * kn, axis=-1, keepdims=True)
+
+    def mix(slot, b, part, s, self_logit):
+        v8 = v_s[pl.ds(pl.multiple_of(b * KV_TOK + part * 8, 8), 8)]
+        vn = jnp.concatenate([v8[:, (h // 2) * 256:(h // 2 + 1) * 256] for h in range(4)], 0)
         peak = jnp.maximum(jnp.max(s, axis=-1, keepdims=True), self_logit)
         w = jnp.exp(s - peak)
         sw = jnp.exp(self_logit - peak)
         inv = 1.0 / (jnp.sum(w, axis=-1, keepdims=True) + sw)
         p = w * inv
         sp = (sw * inv).astype(jnp.bfloat16).astype(jnp.float32)
-        pp = jnp.concatenate([p, jnp.concatenate([p[:, n_key - 2:], p[:, :n_key - 2]], 1)], 0).astype(jnp.bfloat16)
-        o2 = dot(pp, vbuf[slot, rows])
+        pp = jnp.concatenate([p, roll(p, 2)], 0).astype(jnp.bfloat16)
+        o2 = dot(pp, vbuf[slot, pl.ds(part * n_key, n_key)])
         return jnp.concatenate([o2[:32], o2[32:]], 1) + sp * vn
 
     def swiglu(i):
@@ -244,13 +244,20 @@
             gain = jnp.where(layer == other, gains[other:other + 1], gain)
 
         def norm(i, _):
-            r = pl.ds(pl.multiple_of(c * ROWS + i * 32, 32), 32)
-            x = xs[r].astype(jnp.float32)
-            inv = lax.rsqrt(jnp.sum(x * x, axis=-1, keepdims=True) / width + NORM_EPS)
-            a_s[pl.ds(pl.multiple_of(i * 32, 32), 32)] = (x * inv * gain).astype(jnp.bfloat16)
-            return 0
-
-        lax.fori_loop(0, ROWS // 32, norm, 0)
+            src = pl.ds(pl.multiple_of(c * ROWS + i * 16, 16), 16)
+            dst = pl.ds(pl.multiple_of(i * 16, 16), 16)
+            parts = range(0, width, 256)
+            total = jnp.zeros((16, 256), jnp.float32)
+            for p in parts:
+                x = xs[src, p:p + 256].astype(jnp.float32)
+                total = total + x * x
+            inv = lax.rsqrt(jnp.sum(total, axis=-1, keepdims=True) / width + NORM_EPS)
+            for p in parts:
+                x = xs[src, p:p + 256].astype(jnp.float32)
+                a_s[dst, p:p + 256] = (x * inv * gain[:, p:p + 256]).astype(jnp.bfloat16)
+            return 0
+
+        lax.fori_loop(0, ROWS // 16, norm, 0)
 
         @pl.when(st >= 1)
         def _():
@@ -260,29 +267,35 @@
         s0, s1 = w_wait(w0), w_wait(w0 + 1)
         rope(dot(a_s[...], wbuf[s0]), 0, q_s, 0, rows)
         rope(dot(a_s[...], wbuf[s1]), 0, q_s, TILE, rows)
-        w_next(w0)
-        w_next(w0 + 1)
         s0, s1 = w_wait(w0 + 2), w_wait(w0 + 3)
         rope(dot(a_s[...], wbuf[s0]), 0, k_s, 0, rows)
         v_s[...] = dot(a_s[...], wbuf[s1]).astype(jnp.bfloat16).astype(jnp.float32)
-        w_next(w0 + 2)
-        w_next(w0 + 3)
 
         def block(b, _):
             gb = st * n_kv + b
             slot = lax.rem(gb, KV_SLOTS)
             for cp in kv_copies(gb):
                 cp.wait()
-            o0, o1 = attend(slot, b, c, 0), attend(slot, b, c, 1)
+            n_part = KV_TOK // 8
+            ahead, outs = logits(slot, b, c, 0), []
+            for g in range(n_part):
+                now = ahead
+                if g + 1 < n_part:
+                    ahead = logits(slot, b, c, g + 1)
+                outs.append(mix(slot, b, g, *now))
             t = pl.ds(pl.multiple_of(b * KV_TOK, KV_TOK), KV_TOK)
             for h in range(4):
-                o = jnp.concatenate([o0[h * 8:h * 8 + 8], o1[h * 8:h * 8 + 8]], 0)
+                o = jnp.concatenate([part[h * 8:h * 8 + 8] for part in outs], 0)
                 att_s[t, h * 256:(h + 1) * 256] = o.astype(jnp.bfloat16)
 
             @pl.when(gb + KV_SLOTS < all_kv)
             def _():
                 for cp in kv_copies(gb + KV_SLOTS):
                     cp.start()
+
+            @pl.when(b < n_q + 2)
+            def _():
+                w_next(w0 + b)
 
             return 0
 
@@ -307,21 +320,23 @@
 
         def down(j, _):
             gt = w0 + n_q + 2 + 2 * n_ff + j
-            go = st * n_dn + j
             s0 = w_wait(gt)
-            wo_copy(go).wait()
+
+            @pl.when(c == 0)
+            def _():
+                wo_copy(layer, j).wait()
 
             @pl.when(j >= 2)
             def _():
                 chip_sum(par, j - 2)
 
-            ybuf[j] = dot(u_s[...], wbuf[s0]) + dot(att_s[...], wobuf[lax.rem(go, WO_SLOTS)])
+            ybuf[j] = dot(u_s[...], wbuf[s0]) + dot(att_s[...], wobuf[j])
             chip_copy(par, j).start()
             w_next(gt)
 
-            @pl.when(go + WO_SLOTS < all_wo)
+            @pl.when((c == chunks - 1) & (layer < layers - 1))
             def _():
-                wo_copy(go + WO_SLOTS).start()
+                wo_copy(layer + 1, j).start()
 
             return 0
 
@@ -382,14 +397,14 @@
                 pltpu.VMEM((ROWS, TILE), bf),
                 pltpu.VMEM((32, 8 * tok_rows), jnp.int32),
                 pltpu.VMEM((SLOTS, width, TILE), bf),
-                pltpu.VMEM((WO_SLOTS, w_o.shape[1], TILE), bf),
+                pltpu.VMEM((n_dn, w_o.shape[1], TILE), bf),
                 pltpu.VMEM((KV_SLOTS, KV_TOK * tok_rows, half), bf),
                 pltpu.VMEM((KV_SLOTS, KV_TOK * tok_rows, half), bf),
                 pltpu.VMEM((n_dn, ROWS, TILE), f32),
                 pltpu.VMEM((2, n_dn, HALF, TILE), f32),
                 pltpu.VMEM((n_dn, HALF, TILE), bf),
                 pltpu.VMEM((2, n_dn, HALF, TILE), bf),
-                dma((SLOTS,)), dma((WO_SLOTS,)), dma((2, KV_SLOTS)), dma((2,)),
+                dma((SLOTS,)), dma((n_dn,)), dma((2, KV_SLOTS)), dma((2,)),
                 dma((n_dn,)), dma((2, n_dn)), dma((n_dn,)), dma((2, n_dn)), dma((2, n_dn)), dma((2, n_dn)), dma((2,)),
             ],
             compiler_params=pltpu.CompilerParams(

time: 250 us -> 217 us (0.87)
  Pallas kernels: 242 us -> 209 us
    pallas_call x1, Pallas kernels: 242 us -> 209 us  [per_device(): pl.pallas_call(functools.partial(kernel, (layers, tokens, width, seq, kv_...]
where the time goes in v2:
time: 217 us
  Pallas kernels  209 us (96%)
  local copies, waits for them, and re-layouts  5.64 us (3%)
  other arithmetic  2.51 us (1%)
    pallas_call x1, Pallas kernels, per_device(): pl.pallas_call(functools.partial(kernel, (layers, tokens, width, seq, kv_...  209 us

profile of v2, /device:TPU:0, one launch (start us, length us, event | category | flops | bytes accessed | tf_op | source)
XLA Modules:
  0.0 217.0 jit_solution(532829331921756031)
XLA Ops:
  0.0 0.7 convert_element_type.10
  0.7 1.5 copy.17.lens_ref
  2.2 1.8 multiply_sine_fusion
  4.0 208.8 %decoder.1 = bf16[512,3584]{1,0:T(8,128)(2,1)} custom-call(s32[512,1]{1,0:T(8,128)} %copy.17.lens_ref, f32[512,128]{1,0:T(8,128)} %get-tuple-element.6.cos_ref, f32[512,128]{1,0:T(8,128)} %get-tuple-element.5.sin_ref, bf16[2,3584]{1,0:T(2,128)(2,1)} %gain_ref.1, bf16[512,3584]{1,0:T(8,128)(2,1)} %x_in.1, bf16[2,3584,1024]{2,1,0:T(8,128)(2,1)} %wq.1, ...), custom_call_target="tpu_custom_call" | custom-call | tf_op jit(solution)/shard_map/decoder/pallas_call | solution.py:383
  212.9 4.1 %copy.19 = bf16[512,3584]{1,0:T(8,128)(2,1)} copy(bf16[512,3584]{1,0:T(8,128)(2,1)} %decoder.1) | data formatting | bytes 7340032
  (1 shorter events, 0.0 us)

commit v3 on v2

--- a/solution.py
+++ b/solution.py
@@ -15,12 +15,12 @@
 HALF = 128
 TILE = 512
 SLOTS = 7
-KV_SLOTS = 3
-KV_TOK = 32
+KV_SLOTS = 6
+KV_TOK = 16
 
 
 def kernel(cfg, lens_ref, cos_ref, sin_ref, gain_ref, x_in, wq, wk, wv, wo, wg, wu, wd, kc, vc, x_out,
-           xs, a_s, q_s, k_s, v_s, att_s, u_s, graw, uraw, sidx, wbuf, wobuf, kbuf, vbuf, ybuf, irecv, rown, xrecv,
+           xs, a_s, q_s, k_s, v_s, att_s, u_s, raws, sidx, s_s, p_s, o_s, wbuf, wobuf, kbuf, vbuf, ybuf, irecv, rown, xrecv,
            wsem, wosem, kvsem, xsem, isend, irsem, xsend, xrsem, nsend, nrsem, osem):
     layers, tokens, width, seq, kv_heads = cfg
     tok_rows = seq * kv_heads * 2
@@ -175,11 +175,11 @@
     match = (lax.div(lane, tok_rows) == lax.rem(row, 8)) & (lax.rem(lane, kv_heads) == lax.div(row, 16)) & (lax.rem(lane, per) < kv_heads)
     sidx[...] = jnp.where(match, lax.rem(lax.div(lane, per), seq), 2 * seq)
 
-    def rope(y, base, dst, col, rows):
+    def rope(y, dst, col, rows):
         cos, sin = cos_ref[rows], sin_ref[rows]
         for h in range(TILE // 256):
-            first = y[:, h * 256:h * 256 + 128].astype(jnp.bfloat16).astype(jnp.float32)
-            second = y[:, h * 256 + 128:h * 256 + 256].astype(jnp.bfloat16).astype(jnp.float32)
+            first = y[:, h * 256:h * 256 + 128].astype(jnp.float32)
+            second = y[:, h * 256 + 128:h * 256 + 256].astype(jnp.float32)
             at = col + h * 256
             dst[:, at:at + 128] = (first * cos - second * sin).astype(jnp.bfloat16).astype(jnp.float32)
             dst[:, at + 128:at + 256] = (second * cos + first * sin).astype(jnp.bfloat16).astype(jnp.float32)
@@ -192,35 +192,60 @@
     def roll(x, by):
         return jnp.concatenate([pltpu.roll(x[:, i:i + 128], by % 128, axis=1) for i in range(0, n_key, 128)], 1)
 
-    def logits(slot, b, c, part):
-        base = pl.multiple_of(b * KV_TOK + part * 8, 8)
-        q8, k8 = q_s[pl.ds(base, 8)], k_s[pl.ds(base, 8)]
-        q = jnp.concatenate([q8[:, h * 256:(h + 1) * 256] for h in range(4)], 0) * scale
-        kn = jnp.concatenate([k8[:, (h // 2) * 256:(h // 2 + 1) * 256] for h in range(4)], 0)
-        len8 = lens_ref[pl.ds(pl.multiple_of(c * ROWS + base, 8), 8), :]
-        lens = jnp.concatenate([len8] * 4, 0)
-        qq = jnp.concatenate([q[:, :128], q[:, 128:]], 0).astype(jnp.bfloat16)
-        keys = kbuf[slot, pl.ds(part * n_key, n_key)]
-        s2 = lax.dot_general(qq, keys, (((1,), (1,)), ((), ())), preferred_element_type=jnp.float32)
-        s = s2[:32] + roll(s2[32:], -2)
-        return jnp.where(sidx[...] < lens, s, -jnp.inf), jnp.sum(q * kn, axis=-1, keepdims=True)
-
-    def mix(slot, b, part, s, self_logit):
-        v8 = v_s[pl.ds(pl.multiple_of(b * KV_TOK + part * 8, 8), 8)]
-        vn = jnp.concatenate([v8[:, (h // 2) * 256:(h // 2 + 1) * 256] for h in range(4)], 0)
-        peak = jnp.maximum(jnp.max(s, axis=-1, keepdims=True), self_logit)
-        w = jnp.exp(s - peak)
-        sw = jnp.exp(self_logit - peak)
-        inv = 1.0 / (jnp.sum(w, axis=-1, keepdims=True) + sw)
-        p = w * inv
-        sp = (sw * inv).astype(jnp.bfloat16).astype(jnp.float32)
-        pp = jnp.concatenate([p, roll(p, 2)], 0).astype(jnp.bfloat16)
-        o2 = dot(pp, vbuf[slot, pl.ds(part * n_key, n_key)])
-        return jnp.concatenate([o2[:32], o2[32:]], 1) + sp * vn
-
-    def swiglu(i):
-        g = graw[...].astype(jnp.float32)
-        u = uraw[...].astype(jnp.float32)
+    n_part = KV_TOK // 8
+
+    def spread(x8, group):
+        return jnp.concatenate([x8[:, (h // group) * 256:(h // group + 1) * 256] for h in range(4)], 0)
+
+    def logits(side, st, b):
+        slot = lax.rem(st * n_kv + b, KV_SLOTS)
+        for g in range(n_part):
+            q = spread(q_s[pl.ds(pl.multiple_of(b * KV_TOK + g * 8, 8), 8)], 1) * scale
+            qq = jnp.concatenate([q[:, :128], q[:, 128:]], 0).astype(jnp.bfloat16)
+            keys = kbuf[slot, pl.ds(g * n_key, n_key)]
+            s2 = lax.dot_general(qq, keys, (((1,), (1,)), ((), ())), preferred_element_type=jnp.float32)
+            s_s[side][g] = s2
+
+    def soft(side, c, b):
+        for g in range(n_part):
+            base = pl.multiple_of(b * KV_TOK + g * 8, 8)
+            tok = pl.ds(base, 8)
+            self_logit = jnp.sum(spread(q_s[tok], 1) * scale * spread(k_s[tok], 2), axis=-1, keepdims=True)
+            lens = jnp.concatenate([lens_ref[pl.ds(pl.multiple_of(c * ROWS + base, 8), 8), :]] * 4, 0)
+            s = jnp.where(sidx[...] < lens, s_s[side][g, :32] + roll(s_s[side][g, 32:], -2), -jnp.inf)
+            peak = jnp.maximum(jnp.max(s, axis=-1, keepdims=True), self_logit)
+            w = jnp.exp(s - peak)
+            sw = jnp.exp(self_logit - peak)
+            inv = 1.0 / (jnp.sum(w, axis=-1, keepdims=True) + sw)
+            p = w * inv
+            p_s[side][g, :32] = p.astype(jnp.bfloat16)
+            p_s[side][g, 32:] = roll(p, 2).astype(jnp.bfloat16)
+            o_s[side][g] = (sw * inv).astype(jnp.bfloat16).astype(jnp.float32) * spread(v_s[tok], 2)
+
+    def mix(side, st, b):
+        slot = lax.rem(st * n_kv + b, KV_SLOTS)
+        outs = []
+        for g in range(n_part):
+            o2 = dot(p_s[side][g], vbuf[slot, pl.ds(g * n_key, n_key)])
+            outs.append(jnp.concatenate([o2[:32], o2[32:]], 1) + o_s[side][g])
+        t = pl.ds(pl.multiple_of(b * KV_TOK, KV_TOK), KV_TOK)
+        for h in range(4):
+            o = jnp.concatenate([part[h * 8:h * 8 + 8] for part in outs], 0)
+            att_s[t, h * 256:(h + 1) * 256] = o.astype(jnp.bfloat16)
+
+    def k_next(gb):
+        @pl.when(gb + KV_SLOTS < all_kv)
+        def _():
+            kv_copies(gb + KV_SLOTS)[0].start()
+
+    def v_next(gb):
+        @pl.when(gb + KV_SLOTS < all_kv)
+        def _():
+            kv_copies(gb + KV_SLOTS)[1].start()
+
+    def swiglu(side, i):
+        g = raws[2 * side][...].astype(jnp.float32)
+        u = raws[2 * side + 1][...].astype(jnp.float32)
         u_s[:, pl.ds(pl.multiple_of(i * TILE, TILE), TILE)] = (g * (1.0 / (1.0 + jnp.exp(-g))) * u).astype(jnp.bfloat16)
 
     def stage(st, _):
@@ -243,7 +268,7 @@
         for other in range(1, layers):
             gain = jnp.where(layer == other, gains[other:other + 1], gain)
 
-        def norm(i, _):
+        def norm_rows(i):
             src = pl.ds(pl.multiple_of(c * ROWS + i * 16, 16), 16)
             dst = pl.ds(pl.multiple_of(i * 16, 16), 16)
             parts = range(0, width, 256)
@@ -255,64 +280,86 @@
             for p in parts:
                 x = xs[src, p:p + 256].astype(jnp.float32)
                 a_s[dst, p:p + 256] = (x * inv * gain[:, p:p + 256]).astype(jnp.bfloat16)
-            return 0
-
-        lax.fori_loop(0, ROWS // 16, norm, 0)
+
+        def norm(i, _):
+            norm_rows(2 * i)
+            norm_rows(2 * i + 1)
+            return 0
+
+        lax.fori_loop(0, ROWS // 32, norm, 0)
 
         @pl.when(st >= 1)
         def _():
             for j in range(n_dn - 2, n_dn):
                 chip_sum(1 - par, j)
 
-        s0, s1 = w_wait(w0), w_wait(w0 + 1)
-        rope(dot(a_s[...], wbuf[s0]), 0, q_s, 0, rows)
-        rope(dot(a_s[...], wbuf[s1]), 0, q_s, TILE, rows)
-        s0, s1 = w_wait(w0 + 2), w_wait(w0 + 3)
-        rope(dot(a_s[...], wbuf[s0]), 0, k_s, 0, rows)
-        v_s[...] = dot(a_s[...], wbuf[s1]).astype(jnp.bfloat16).astype(jnp.float32)
-
-        def block(b, _):
-            gb = st * n_kv + b
-            slot = lax.rem(gb, KV_SLOTS)
-            for cp in kv_copies(gb):
-                cp.wait()
-            n_part = KV_TOK // 8
-            ahead, outs = logits(slot, b, c, 0), []
-            for g in range(n_part):
-                now = ahead
-                if g + 1 < n_part:
-                    ahead = logits(slot, b, c, g + 1)
-                outs.append(mix(slot, b, g, *now))
-            t = pl.ds(pl.multiple_of(b * KV_TOK, KV_TOK), KV_TOK)
-            for h in range(4):
-                o = jnp.concatenate([part[h * 8:h * 8 + 8] for part in outs], 0)
-                att_s[t, h * 256:(h + 1) * 256] = o.astype(jnp.bfloat16)
-
-            @pl.when(gb + KV_SLOTS < all_kv)
+        slots = [w_wait(w0), w_wait(w0 + 1)]
+        for i in range(2):
+            raws[i][...] = dot(a_s[...], wbuf[slots[i]]).astype(jnp.bfloat16)
+        w_next(w0)
+        w_next(w0 + 1)
+        slots = [w_wait(w0 + 2), w_wait(w0 + 3)]
+        raws[2][...] = dot(a_s[...], wbuf[slots[0]]).astype(jnp.bfloat16)
+        rope(raws[0], q_s, 0, rows)
+        rope(raws[1], q_s, TILE, rows)
+        v_s[...] = dot(a_s[...], wbuf[slots[1]]).astype(jnp.bfloat16).astype(jnp.float32)
+        rope(raws[2], k_s, 0, rows)
+
+        b0 = st * n_kv
+        kv_copies(b0)[0].wait()
+        logits(0, st, 0)
+        k_next(b0)
+        kv_copies(b0 + 1)[0].wait()
+        soft(0, c, 0)
+        logits(1, st, 1)
+        k_next(b0 + 1)
+
+        def half(side, b):
+            kv_copies(b0 + b - 1)[1].wait()
+            kv_copies(b0 + b + 1)[0].wait()
+            mix(1 - side, st, b - 1)
+            soft(side, c, b)
+            logits(1 - side, st, b + 1)
+            v_next(b0 + b - 1)
+            k_next(b0 + b + 1)
+
+        def block(i, _):
+            half(1, 2 * i + 1)
+
+            @pl.when((i == 0) | (i == 2))
             def _():
-                for cp in kv_copies(gb + KV_SLOTS):
-                    cp.start()
-
-            @pl.when(b < n_q + 2)
-            def _():
-                w_next(w0 + b)
-
-            return 0
-
-        lax.fori_loop(0, n_kv, block, 0)
-
-        def ff(i, _):
+                w_next(w0 + n_q + lax.div(i, 2))
+
+            half(0, 2 * i + 2)
+            return 0
+
+        lax.fori_loop(0, n_kv // 2 - 1, block, 0)
+        kv_copies(b0 + n_kv - 2)[1].wait()
+        mix(0, st, n_kv - 2)
+        soft(1, c, n_kv - 1)
+        v_next(b0 + n_kv - 2)
+        kv_copies(b0 + n_kv - 1)[1].wait()
+        mix(1, st, n_kv - 1)
+        v_next(b0 + n_kv - 1)
+
+        def ff_tile(side, i):
             gt = w0 + n_q + 2 + 2 * i
             s0, s1 = w_wait(gt), w_wait(gt + 1)
-            swiglu(lax.rem(i + n_ff - 1, n_ff))
-            graw[...] = dot(a_s[...], wbuf[s0]).astype(jnp.bfloat16)
-            uraw[...] = dot(a_s[...], wbuf[s1]).astype(jnp.bfloat16)
+            swiglu(1 - side, lax.rem(i + n_ff - 1, n_ff))
+            raws[2 * side][...] = dot(a_s[...], wbuf[s0]).astype(jnp.bfloat16)
+            raws[2 * side + 1][...] = dot(a_s[...], wbuf[s1]).astype(jnp.bfloat16)
             w_next(gt)
             w_next(gt + 1)
-            return 0
-
-        lax.fori_loop(0, n_ff, ff, 0)
-        swiglu(n_ff - 1)
+
+        def ff(i, _):
+            ff_tile(0, 2 * i)
+            ff_tile(1, 2 * i + 1)
+            return 0
+
+        lax.fori_loop(0, n_ff // 2, ff, 0)
+        if n_ff % 2:
+            ff_tile(0, n_ff - 1)
+        swiglu((n_ff - 1) % 2, n_ff - 1)
 
         @pl.when(st >= 1)
         def _():
@@ -343,8 +390,8 @@
         lax.fori_loop(0, n_dn, down, 0)
         return 0
 
-    graw[...] = jnp.zeros_like(graw)
-    uraw[...] = jnp.zeros_like(uraw)
+    for raw in raws:
+        raw[...] = jnp.zeros_like(raw)
     lax.fori_loop(0, stages, stage, 0)
 
     last = (stages - 1) % chunks
@@ -393,9 +440,11 @@
                 pltpu.VMEM((ROWS, w_v.shape[2]), f32),
                 pltpu.VMEM((ROWS, w_q.shape[2]), bf),
                 pltpu.VMEM((ROWS, w_gate.shape[2]), bf),
-                pltpu.VMEM((ROWS, TILE), bf),
-                pltpu.VMEM((ROWS, TILE), bf),
+                [pltpu.VMEM((ROWS, TILE), bf)] * 4,
                 pltpu.VMEM((32, 8 * tok_rows), jnp.int32),
+                [pltpu.VMEM((KV_TOK // 8, 64, 8 * tok_rows), f32)] * 2,
+                [pltpu.VMEM((KV_TOK // 8, 64, 8 * tok_rows), bf)] * 2,
+                [pltpu.VMEM((KV_TOK // 8, 32, head), f32)] * 2,
                 pltpu.VMEM((SLOTS, width, TILE), bf),
                 pltpu.VMEM((n_dn, w_o.shape[1], TILE), bf),
                 pltpu.VMEM((KV_SLOTS, KV_TOK * tok_rows, half), bf),

time: 217 us -> 199 us (0.917)
  Pallas kernels: 209 us -> 190 us
    pallas_call x1, Pallas kernels: 209 us -> 190 us  [per_device(): pl.pallas_call(functools.partial(kernel, (layers, tokens, width, seq, kv_...]
where the time goes in v3:
time: 199 us
  Pallas kernels  190 us (95%)
  local copies, waits for them, and re-layouts  5.64 us (3%)
  other arithmetic  2.51 us (1%)
    pallas_call x1, Pallas kernels, per_device(): pl.pallas_call(functools.partial(kernel, (layers, tokens, width, seq, kv_...  190 us
    unnamed x1, local copies, waits for them, and re-layouts  4.11 us

profile of v3, /device:TPU:0, one launch (start us, length us, event | category | flops | bytes accessed | tf_op | source)
XLA Modules:
  0.0 198.7 jit_solution(9099697247733477022)
XLA Ops:
  0.0 0.7 convert_element_type.10
  0.7 1.5 copy.17.lens_ref
  2.2 1.8 multiply_sine_fusion
  4.0 190.5 %decoder.1 = bf16[512,3584]{1,0:T(8,128)(2,1)} custom-call(s32[512,1]{1,0:T(8,128)} %copy.17.lens_ref, f32[512,128]{1,0:T(8,128)} %get-tuple-element.6.cos_ref, f32[512,128]{1,0:T(8,128)} %get-tuple-element.5.sin_ref, bf16[2,3584]{1,0:T(2,128)(2,1)} %gain_ref.1, bf16[512,3584]{1,0:T(8,128)(2,1)} %x_in.1, bf16[2,3584,1024]{2,1,0:T(8,128)(2,1)} %wq.1, ...), custom_call_target="tpu_custom_call" | custom-call | tf_op jit(solution)/shard_map/decoder/pallas_call | solution.py:430
  194.5 4.1 %copy.19 = bf16[512,3584]{1,0:T(8,128)(2,1)} copy(bf16[512,3584]{1,0:T(8,128)(2,1)} %decoder.1) | data formatting | bytes 7340032
  (1 shorter events, 0.0 us)

commit v4 on v3

--- a/solution.py
+++ b/solution.py
@@ -2,6 +2,7 @@
 
 import jax
 import jax.numpy as jnp
+import numpy as np
 from jax import lax
 from jax.experimental import pallas as pl
 from jax.experimental.pallas import tpu as pltpu
@@ -15,12 +16,13 @@
 HALF = 128
 TILE = 512
 SLOTS = 7
-KV_SLOTS = 6
+KV_SLOTS = 9
+X_SLOTS = 4
 KV_TOK = 16
 
 
-def kernel(cfg, lens_ref, cos_ref, sin_ref, gain_ref, x_in, wq, wk, wv, wo, wg, wu, wd, kc, vc, x_out,
-           xs, a_s, q_s, k_s, v_s, att_s, u_s, raws, sidx, s_s, p_s, o_s, wbuf, wobuf, kbuf, vbuf, ybuf, irecv, rown, xrecv,
+def kernel(cfg, lens_ref, table_ref, gain_ref, x_in, wq, wk, wv, wo, wg, wu, wd, kc, vc, x_out,
+           xs, a_s, q_s, k_s, v_s, att_s, u_s, raws, cos_ref, sin_ref, len_s, sidx, s_s, p_s, o_s, wbuf, wobuf, kbuf, vbuf, ybuf, irecv, rown, xrecv,
            wsem, wosem, kvsem, xsem, isend, irsem, xsend, xrsem, nsend, nrsem, osem):
     layers, tokens, width, seq, kv_heads = cfg
     tok_rows = seq * kv_heads * 2
@@ -102,10 +104,11 @@
         return (pltpu.make_async_copy(kc.at[rows], kbuf.at[slot], kvsem.at[0, slot]),
                 pltpu.make_async_copy(vc.at[rows], vbuf.at[slot], kvsem.at[1, slot]))
 
-    def chip_copy(par, j):
+    def chip_copy(gj):
+        slot = lax.rem(gj, X_SLOTS)
         return pltpu.make_async_remote_copy(
-            src_ref=ybuf.at[j, pl.ds(sib_row, HALF)], dst_ref=irecv.at[par, j], send_sem=isend.at[j],
-            recv_sem=irsem.at[par, j], device_id={"tp": sib}, device_id_type=MESH)
+            src_ref=ybuf.at[slot, pl.ds(sib_row, HALF)], dst_ref=irecv.at[slot], send_sem=isend.at[slot],
+            recv_sem=irsem.at[slot], device_id={"tp": sib}, device_id_type=MESH)
 
     def link_copy(par, j):
         return pltpu.make_async_remote_copy(
@@ -121,15 +124,16 @@
             src_ref=piece, dst_ref=piece, send_sem=nsend.at[par, j],
             recv_sem=nrsem.at[par, j], device_id={"tp": sib}, device_id_type=MESH)
 
-    def chip_sum(par, j):
-        chip_copy(par, j).wait_recv()
-        rown[j] = (ybuf[j, pl.ds(own_row, HALF)] + irecv[par, j]).astype(jnp.bfloat16)
-        link_copy(par, j).start()
+    def chip_sum(st, j):
+        gj = st * n_dn + j
+        slot = lax.rem(gj, X_SLOTS)
+        chip_copy(gj).wait()
+        rown[j] = (ybuf[slot, pl.ds(own_row, HALF)] + irecv[slot]).astype(jnp.bfloat16)
+        link_copy(lax.rem(st, chunks), j).start()
 
     def finish(par):
         def step(j, _):
             link_copy(par, j).wait()
-            chip_copy(par, j).wait_send()
             piece = x_piece(par, own_row, j)
             total = rown[j].astype(jnp.float32) + xrecv[par, j].astype(jnp.float32)
             piece[...] = (piece[...].astype(jnp.float32) + total).astype(jnp.bfloat16)
@@ -153,8 +157,7 @@
         rows = pl.ds(c * ROWS, ROWS)
         return pltpu.make_async_copy(xs.at[rows], x_out.at[rows], osem.at[c])
 
-    for c in range(chunks):
-        x_copy(c).start()
+    x_copy(0).start()
     for g in range(SLOTS):
         w_start(jnp.int32(g))
     for g in range(KV_SLOTS):
@@ -162,6 +165,8 @@
             cp.start()
     for j in range(n_dn):
         wo_copy(0, j).start()
+    for c in range(1, chunks):
+        x_copy(c).start()
 
     barrier = pltpu.get_barrier_semaphore()
     for other in (sib, partner):
@@ -173,7 +178,12 @@
     row = lax.broadcasted_iota(jnp.int32, (32, n_key), 0)
     per = 2 * kv_heads
     match = (lax.div(lane, tok_rows) == lax.rem(row, 8)) & (lax.rem(lane, kv_heads) == lax.div(row, 16)) & (lax.rem(lane, per) < kv_heads)
-    sidx[...] = jnp.where(match, lax.rem(lax.div(lane, per), seq), 2 * seq)
+    sidx[...] = jnp.where(match, lax.rem(lax.div(lane, per), seq), 2 * seq).astype(jnp.float32)
+    pick = lax.broadcasted_iota(jnp.int32, (seq, tokens), 0) == lens_ref[...]
+    angles = lax.dot_general(pick.astype(jnp.float32), table_ref[...], (((0,), (0,)), ((), ())),
+                             precision=lax.Precision.HIGHEST, preferred_element_type=jnp.float32)
+    half = angles.shape[1] // 3
+    cos_ref[...], sin_ref[...], len_s[...] = angles[:, :half], angles[:, half:2 * half], angles[:, 2 * half:]
 
     def rope(y, dst, col, rows):
         cos, sin = cos_ref[rows], sin_ref[rows]
@@ -211,7 +221,7 @@
             base = pl.multiple_of(b * KV_TOK + g * 8, 8)
             tok = pl.ds(base, 8)
             self_logit = jnp.sum(spread(q_s[tok], 1) * scale * spread(k_s[tok], 2), axis=-1, keepdims=True)
-            lens = jnp.concatenate([lens_ref[pl.ds(pl.multiple_of(c * ROWS + base, 8), 8), :]] * 4, 0)
+            lens = jnp.concatenate([len_s[pl.ds(pl.multiple_of(c * ROWS + base, 8), 8), :1]] * 4, 0)
             s = jnp.where(sidx[...] < lens, s_s[side][g, :32] + roll(s_s[side][g, 32:], -2), -jnp.inf)
             peak = jnp.maximum(jnp.max(s, axis=-1, keepdims=True), self_logit)
             w = jnp.exp(s - peak)
@@ -291,7 +301,7 @@
         @pl.when(st >= 1)
         def _():
             for j in range(n_dn - 2, n_dn):
-                chip_sum(1 - par, j)
+                chip_sum(st - 1, j)
 
         slots = [w_wait(w0), w_wait(w0 + 1)]
         for i in range(2):
@@ -375,10 +385,11 @@
 
             @pl.when(j >= 2)
             def _():
-                chip_sum(par, j - 2)
-
-            ybuf[j] = dot(u_s[...], wbuf[s0]) + dot(att_s[...], wobuf[j])
-            chip_copy(par, j).start()
+                chip_sum(st, j - 2)
+
+            gj = st * n_dn + j
+            ybuf[lax.rem(gj, X_SLOTS)] = dot(u_s[...], wbuf[s0]) + dot(att_s[...], wobuf[j])
+            chip_copy(gj).start()
             w_next(gt)
 
             @pl.when((c == chunks - 1) & (layer < layers - 1))
@@ -396,7 +407,7 @@
 
     last = (stages - 1) % chunks
     for j in range(n_dn - 2, n_dn):
-        chip_sum(last, j)
+        chip_sum(stages - 1, j)
     new_wait(1 - last)
     out_copy(1 - last).start()
     finish(last)
@@ -413,9 +424,10 @@
         layers, tokens, seq, kv_heads, head = k_cache.shape
         width = x_in.shape[1]
         half = head // 2
-        inv_freq = 1.0 / (ROPE_BASE ** (jnp.arange(0, head, 2).astype(jnp.float32) / head))
-        angles = lengths.astype(jnp.float32)[:, None] * inv_freq[None, :]
-        cos, sin = jnp.cos(angles), jnp.sin(angles)
+        inv_freq = 1.0 / (np.float32(ROPE_BASE) ** (np.arange(0, head, 2).astype(np.float32) / np.float32(head)))
+        pos = np.arange(seq).astype(np.float32)[:, None]
+        angles = pos * inv_freq[None, :].astype(np.float32)
+        table = np.concatenate([np.cos(angles), np.sin(angles), pos + 0 * angles], 1).astype(np.float32)
 
         def rows_of(cache):
             r = cache.reshape(layers * tokens * seq, kv_heads, 2, half).transpose(0, 2, 1, 3)
@@ -430,7 +442,7 @@
         return pl.pallas_call(
             functools.partial(kernel, (layers, tokens, width, seq, kv_heads)),
             out_shape=jax.ShapeDtypeStruct(x_in.shape, bf),
-            in_specs=[vm] * 4 + [hbm] * 10,
+            in_specs=[vm] * 3 + [hbm] * 10,
             out_specs=hbm,
             scratch_shapes=[
                 pltpu.VMEM((tokens, width), bf),
@@ -441,7 +453,10 @@
                 pltpu.VMEM((ROWS, w_q.shape[2]), bf),
                 pltpu.VMEM((ROWS, w_gate.shape[2]), bf),
                 [pltpu.VMEM((ROWS, TILE), bf)] * 4,
-                pltpu.VMEM((32, 8 * tok_rows), jnp.int32),
+                pltpu.VMEM((tokens, half), f32),
+                pltpu.VMEM((tokens, half), f32),
+                pltpu.VMEM((tokens, half), f32),
+                pltpu.VMEM((32, 8 * tok_rows), f32),
                 [pltpu.VMEM((KV_TOK // 8, 64, 8 * tok_rows), f32)] * 2,
                 [pltpu.VMEM((KV_TOK // 8, 64, 8 * tok_rows), bf)] * 2,
                 [pltpu.VMEM((KV_TOK // 8, 32, head), f32)] * 2,
@@ -449,17 +464,17 @@
                 pltpu.VMEM((n_dn, w_o.shape[1], TILE), bf),
                 pltpu.VMEM((KV_SLOTS, KV_TOK * tok_rows, half), bf),
                 pltpu.VMEM((KV_SLOTS, KV_TOK * tok_rows, half), bf),
-                pltpu.VMEM((n_dn, ROWS, TILE), f32),
-                pltpu.VMEM((2, n_dn, HALF, TILE), f32),
+                pltpu.VMEM((X_SLOTS, ROWS, TILE), f32),
+                pltpu.VMEM((X_SLOTS, HALF, TILE), f32),
                 pltpu.VMEM((n_dn, HALF, TILE), bf),
                 pltpu.VMEM((2, n_dn, HALF, TILE), bf),
                 dma((SLOTS,)), dma((n_dn,)), dma((2, KV_SLOTS)), dma((2,)),
-                dma((n_dn,)), dma((2, n_dn)), dma((n_dn,)), dma((2, n_dn)), dma((2, n_dn)), dma((2, n_dn)), dma((2,)),
+                dma((X_SLOTS,)), dma((X_SLOTS,)), dma((n_dn,)), dma((2, n_dn)), dma((2, n_dn)), dma((2, n_dn)), dma((2,)),
             ],
             compiler_params=pltpu.CompilerParams(
                 collective_id=0, has_side_effects=True, vmem_limit_bytes=67_043_328),
             name="decoder",
-        )(lengths[:, None], cos, sin, norm_gain, x_in, w_q, w_k, w_v, w_o, w_gate, w_up, w_down,
+        )(lengths.reshape(1, tokens), jnp.asarray(table), norm_gain, x_in, w_q, w_k, w_v, w_o, w_gate, w_up, w_down,
           rows_of(k_cache), rows_of(v_cache))
 
     return jax.shard_map(per_device, mesh=mesh, in_specs=arg_specs, out_specs=P('dp', None), check_vma=False)

time: 199 us -> 195 us (0.980)
  other arithmetic: 2.51 us -> 0 us
where the time goes in v4:
time: 195 us
  Pallas kernels  191 us (98%)
  local copies, waits for them, and re-layouts  4.11 us (2%)
    pallas_call x1, Pallas kernels, per_device(): pl.pallas_call(functools.partial(kernel, (layers, tokens, width, seq, kv_...  191 us
    unnamed x1, local copies, waits for them, and re-layouts  4.11 us

profile of v4, /device:TPU:0, one launch (start us, length us, event | category | flops | bytes accessed | tf_op | source)
XLA Modules:
  0.0 195.1 jit_solution(405922095058741903)
XLA Ops:
  0.0 191.0 %decoder.1 = bf16[512,3584]{1,0:T(8,128)(2,1)} custom-call(s32[1,512]{1,0:T(1,128)} %bitcast.13, f32[32,384]{1,0:T(8,128)} %constant.2.clone.table_ref, bf16[2,3584]{1,0:T(2,128)(2,1)} %gain_ref.1, bf16[512,3584]{1,0:T(8,128)(2,1)} %x_in.1, bf16[2,3584,1024]{2,1,0:T(8,128)(2,1)} %wq.1, bf16[2,3584,512]{2,1,0:T(8,128)(2,1)} %wk.1, bf16[2,3584,512]{2,1,0:T(8,128)(2,1)} %wv.1, ...), custom_call_target="tpu_custom_call" | custom-call | tf_op jit(solution)/shard_map/decoder/pallas_call | solution.py:442
  191.0 4.1 %copy.17 = bf16[512,3584]{1,0:T(8,128)(2,1)} copy(bf16[512,3584]{1,0:T(8,128)(2,1)} %decoder.1) | data formatting | bytes 7340032

commit v5 on v4

--- a/solution.py
+++ b/solution.py
@@ -16,13 +16,13 @@
 HALF = 128
 TILE = 512
 SLOTS = 7
-KV_SLOTS = 9
+KV_SLOTS = 7
 X_SLOTS = 4
 KV_TOK = 16
 
 
 def kernel(cfg, lens_ref, table_ref, gain_ref, x_in, wq, wk, wv, wo, wg, wu, wd, kc, vc, x_out,
-           xs, a_s, q_s, k_s, v_s, att_s, u_s, raws, cos_ref, sin_ref, len_s, sidx, s_s, p_s, o_s, wbuf, wobuf, kbuf, vbuf, ybuf, irecv, rown, xrecv,
+           xs, a_s, q_s, k_s, v_s, att_s, u_s, raws, cos_ref, sin_ref, len_s, len4, sidx, s_s, p_s, o_s, wbuf, wobuf, kbuf, vbuf, ybuf, irecv, rown, xrecv,
            wsem, wosem, kvsem, xsem, isend, irsem, xsend, xrsem, nsend, nrsem, osem):
     layers, tokens, width, seq, kv_heads = cfg
     tok_rows = seq * kv_heads * 2
@@ -173,11 +173,11 @@
         pl.semaphore_signal(barrier, inc=1, device_id={"tp": other}, device_id_type=MESH)
     pl.semaphore_wait(barrier, 2)
 
-    n_key = 8 * tok_rows
-    lane = lax.broadcasted_iota(jnp.int32, (32, n_key), 1)
-    row = lax.broadcasted_iota(jnp.int32, (32, n_key), 0)
+    n_key = 2 * tok_rows
+    lane = lax.broadcasted_iota(jnp.int32, (KV_TOK * 4, n_key), 1)
+    row = lax.rem(lax.broadcasted_iota(jnp.int32, (KV_TOK * 4, n_key), 0), 8)
     per = 2 * kv_heads
-    match = (lax.div(lane, tok_rows) == lax.rem(row, 8)) & (lax.rem(lane, kv_heads) == lax.div(row, 16)) & (lax.rem(lane, per) < kv_heads)
+    match = (lax.div(lane, tok_rows) == lax.div(row, 4)) & (lax.rem(lane, kv_heads) == lax.div(lax.rem(row, 4), 2)) & (lax.rem(lane, per) < kv_heads)
     sidx[...] = jnp.where(match, lax.rem(lax.div(lane, per), seq), 2 * seq).astype(jnp.float32)
     pick = lax.broadcasted_iota(jnp.int32, (seq, tokens), 0) == lens_ref[...]
     angles = lax.dot_general(pick.astype(jnp.float32), table_ref[...], (((0,), (0,)), ((), ())),
@@ -185,63 +185,65 @@
     half = angles.shape[1] // 3
     cos_ref[...], sin_ref[...], len_s[...] = angles[:, :half], angles[:, half:2 * half], angles[:, 2 * half:]
 
-    def rope(y, dst, col, rows):
+    def rope(y, dst, first_head, copies, rows):
         cos, sin = cos_ref[rows], sin_ref[rows]
         for h in range(TILE // 256):
             first = y[:, h * 256:h * 256 + 128].astype(jnp.float32)
             second = y[:, h * 256 + 128:h * 256 + 256].astype(jnp.float32)
-            at = col + h * 256
-            dst[:, at:at + 128] = (first * cos - second * sin).astype(jnp.bfloat16).astype(jnp.float32)
-            dst[:, at + 128:at + 256] = (second * cos + first * sin).astype(jnp.bfloat16).astype(jnp.float32)
+            lo = (first * cos - second * sin).astype(jnp.bfloat16).astype(jnp.float32)
+            hi = (second * cos + first * sin).astype(jnp.bfloat16).astype(jnp.float32)
+            for i in range(copies):
+                at = pl.ds((first_head + h) * copies + i, ROWS, 4)
+                dst[0, at] = lo
+                dst[1, at] = hi
 
     def dot(a, b):
         return jnp.dot(a, b, preferred_element_type=jnp.float32)
 
     scale = 1.0 / 16.0
+    n_pair = KV_TOK // 2
+    n_row = KV_TOK * 4
 
     def roll(x, by):
-        return jnp.concatenate([pltpu.roll(x[:, i:i + 128], by % 128, axis=1) for i in range(0, n_key, 128)], 1)
-
-    n_part = KV_TOK // 8
-
-    def spread(x8, group):
-        return jnp.concatenate([x8[:, (h // group) * 256:(h // group + 1) * 256] for h in range(4)], 0)
+        return jnp.concatenate([pltpu.roll(x[:, i:i + 128], by % 128, axis=1) for i in (0, 128)], 1)
+
+    def block_rows(b):
+        return pl.ds(pl.multiple_of(b * n_row, n_row), n_row)
 
     def logits(side, st, b):
         slot = lax.rem(st * n_kv + b, KV_SLOTS)
-        for g in range(n_part):
-            q = spread(q_s[pl.ds(pl.multiple_of(b * KV_TOK + g * 8, 8), 8)], 1) * scale
-            qq = jnp.concatenate([q[:, :128], q[:, 128:]], 0).astype(jnp.bfloat16)
+        q = [(q_s[j, block_rows(b)] * scale).reshape(n_pair, 8, 128) for j in range(2)]
+        qq = jnp.concatenate(q, 1).astype(jnp.bfloat16)
+        for g in range(n_pair):
             keys = kbuf[slot, pl.ds(g * n_key, n_key)]
-            s2 = lax.dot_general(qq, keys, (((1,), (1,)), ((), ())), preferred_element_type=jnp.float32)
-            s_s[side][g] = s2
+            s_s[side][g * 16:g * 16 + 16] = lax.dot_general(
+                qq[g], keys, (((1,), (1,)), ((), ())), preferred_element_type=jnp.float32)
 
     def soft(side, c, b):
-        for g in range(n_part):
-            base = pl.multiple_of(b * KV_TOK + g * 8, 8)
-            tok = pl.ds(base, 8)
-            self_logit = jnp.sum(spread(q_s[tok], 1) * scale * spread(k_s[tok], 2), axis=-1, keepdims=True)
-            lens = jnp.concatenate([len_s[pl.ds(pl.multiple_of(c * ROWS + base, 8), 8), :1]] * 4, 0)
-            s = jnp.where(sidx[...] < lens, s_s[side][g, :32] + roll(s_s[side][g, 32:], -2), -jnp.inf)
-            peak = jnp.maximum(jnp.max(s, axis=-1, keepdims=True), self_logit)
-            w = jnp.exp(s - peak)
-            sw = jnp.exp(self_logit - peak)
-            inv = 1.0 / (jnp.sum(w, axis=-1, keepdims=True) + sw)
-            p = w * inv
-            p_s[side][g, :32] = p.astype(jnp.bfloat16)
-            p_s[side][g, 32:] = roll(p, 2).astype(jnp.bfloat16)
-            o_s[side][g] = (sw * inv).astype(jnp.bfloat16).astype(jnp.float32) * spread(v_s[tok], 2)
+        s2 = s_s[side][...].reshape(n_pair, 2, 8, n_key)
+        s = s2[:, 0].reshape(n_row, n_key) + roll(s2[:, 1].reshape(n_row, n_key), -2)
+        r = block_rows(b)
+        self_logit = jnp.sum(q_s[0, r] * k_s[0, r] + q_s[1, r] * k_s[1, r], axis=-1, keepdims=True) * scale
+        keep = sidx[...] < len4[r, :1]
+        s = jnp.where(keep, s, -jnp.inf)
+        peak = jnp.maximum(jnp.max(s, axis=-1, keepdims=True), self_logit)
+        w = jnp.exp(s - peak)
+        sw = jnp.exp(self_logit - peak)
+        inv = 1.0 / (jnp.sum(w, axis=-1, keepdims=True) + sw)
+        p = w * inv
+        pp = jnp.concatenate([p.reshape(n_pair, 8, n_key), roll(p, 2).reshape(n_pair, 8, n_key)], 1)
+        p_s[side][...] = pp.reshape(2 * n_row, n_key).astype(jnp.bfloat16)
+        sp = (sw * inv).astype(jnp.bfloat16).astype(jnp.float32)
+        for j in range(2):
+            o_s[side][j] = sp * v_s[j, r]
 
     def mix(side, st, b):
         slot = lax.rem(st * n_kv + b, KV_SLOTS)
-        outs = []
-        for g in range(n_part):
-            o2 = dot(p_s[side][g], vbuf[slot, pl.ds(g * n_key, n_key)])
-            outs.append(jnp.concatenate([o2[:32], o2[32:]], 1) + o_s[side][g])
-        t = pl.ds(pl.multiple_of(b * KV_TOK, KV_TOK), KV_TOK)
-        for h in range(4):
-            o = jnp.concatenate([part[h * 8:h * 8 + 8] for part in outs], 0)
-            att_s[t, h * 256:(h + 1) * 256] = o.astype(jnp.bfloat16)
+        base = pl.multiple_of(b * n_row, n_row)
+        for g in range(n_pair):
+            o2 = dot(p_s[side][g * 16:g * 16 + 16], vbuf[slot, pl.ds(g * n_key, n_key)])
+            for j in range(2):
+                q_s[j, pl.ds(base + g * 8, 8)] = o2[j * 8:j * 8 + 8] + o_s[side][j, g * 8:g * 8 + 8]
 
     def k_next(gb):
         @pl.when(gb + KV_SLOTS < all_kv)
@@ -310,10 +312,14 @@
         w_next(w0 + 1)
         slots = [w_wait(w0 + 2), w_wait(w0 + 3)]
         raws[2][...] = dot(a_s[...], wbuf[slots[0]]).astype(jnp.bfloat16)
-        rope(raws[0], q_s, 0, rows)
-        rope(raws[1], q_s, TILE, rows)
-        v_s[...] = dot(a_s[...], wbuf[slots[1]]).astype(jnp.bfloat16).astype(jnp.float32)
-        rope(raws[2], k_s, 0, rows)
+        rope(raws[0], q_s, 0, 1, rows)
+        rope(raws[1], q_s, 2, 1, rows)
+        v = dot(a_s[...], wbuf[slots[1]]).astype(jnp.bfloat16).astype(jnp.float32)
+        rope(raws[2], k_s, 0, 2, rows)
+        for h in range(4):
+            for j in range(2):
+                v_s[j, pl.ds(h, ROWS, 4)] = v[:, (h // 2) * 256 + j * 128:(h // 2) * 256 + j * 128 + 128]
+            len4[pl.ds(h, ROWS, 4)] = len_s[rows]
 
         b0 = st * n_kv
         kv_copies(b0)[0].wait()
@@ -351,6 +357,10 @@
         kv_copies(b0 + n_kv - 1)[1].wait()
         mix(1, st, n_kv - 1)
         v_next(b0 + n_kv - 1)
+        for h in range(4):
+            for j in range(2):
+                at = h * 256 + j * 128
+                att_s[:, at:at + 128] = q_s[j, pl.ds(h, ROWS, 4)].astype(jnp.bfloat16)
 
         def ff_tile(side, i):
             gt = w0 + n_q + 2 + 2 * i
@@ -447,19 +457,20 @@
             scratch_shapes=[
                 pltpu.VMEM((tokens, width), bf),
                 pltpu.VMEM((ROWS, width), bf),
-                pltpu.VMEM((ROWS, w_q.shape[2]), f32),
-                pltpu.VMEM((ROWS, w_k.shape[2]), f32),
-                pltpu.VMEM((ROWS, w_v.shape[2]), f32),
+                pltpu.VMEM((2, 4 * ROWS, half), f32),
+                pltpu.VMEM((2, 4 * ROWS, half), f32),
+                pltpu.VMEM((2, 4 * ROWS, half), f32),
                 pltpu.VMEM((ROWS, w_q.shape[2]), bf),
                 pltpu.VMEM((ROWS, w_gate.shape[2]), bf),
                 [pltpu.VMEM((ROWS, TILE), bf)] * 4,
                 pltpu.VMEM((tokens, half), f32),
                 pltpu.VMEM((tokens, half), f32),
                 pltpu.VMEM((tokens, half), f32),
-                pltpu.VMEM((32, 8 * tok_rows), f32),
-                [pltpu.VMEM((KV_TOK // 8, 64, 8 * tok_rows), f32)] * 2,
-                [pltpu.VMEM((KV_TOK // 8, 64, 8 * tok_rows), bf)] * 2,
-                [pltpu.VMEM((KV_TOK // 8, 32, head), f32)] * 2,
+                pltpu.VMEM((4 * ROWS, half), f32),
+                pltpu.VMEM((4 * KV_TOK, 2 * tok_rows), f32),
+                [pltpu.VMEM((8 * KV_TOK, 2 * tok_rows), f32)] * 2,
+                [pltpu.VMEM((8 * KV_TOK, 2 * tok_rows), bf)] * 2,
+                [pltpu.VMEM((2, 4 * KV_TOK, half), f32)] * 2,
                 pltpu.VMEM((SLOTS, width, TILE), bf),
                 pltpu.VMEM((n_dn, w_o.shape[1], TILE), bf),
                 pltpu.VMEM((KV_SLOTS, KV_TOK * tok_rows, half), bf),

time: 195 us -> 189 us (0.969)
  Pallas kernels: 191 us -> 185 us
    pallas_call x1, Pallas kernels: 191 us -> 185 us  [per_device(): pl.pallas_call(functools.partial(kernel, (layers, tokens, width, seq, kv_...]
where the time goes in v5:
time: 189 us
  Pallas kernels  185 us (98%)
  local copies, waits for them, and re-layouts  4.11 us (2%)
    pallas_call x1, Pallas kernels, per_device(): pl.pallas_call(functools.partial(kernel, (layers, tokens, width, seq, kv_...  185 us
    unnamed x1, local copies, waits for them, and re-layouts  4.11 us

profile of v5, /device:TPU:0, one launch (start us, length us, event | category | flops | bytes accessed | tf_op | source)
XLA Modules:
  0.0 188.9 jit_solution(14223612836517634053)
XLA Ops:
  0.0 184.7 %decoder.1 = bf16[512,3584]{1,0:T(8,128)(2,1)} custom-call(s32[1,512]{1,0:T(1,128)} %bitcast.13, f32[32,384]{1,0:T(8,128)} %constant.2.clone.table_ref, bf16[2,3584]{1,0:T(2,128)(2,1)} %gain_ref.1, bf16[512,3584]{1,0:T(8,128)(2,1)} %x_in.1, bf16[2,3584,1024]{2,1,0:T(8,128)(2,1)} %wq.1, bf16[2,3584,512]{2,1,0:T(8,128)(2,1)} %wk.1, bf16[2,3584,512]{2,1,0:T(8,128)(2,1)} %wv.1, ...), custom_call_target="tpu_custom_call" | custom-call | tf_op jit(solution)/shard_map/decoder/pallas_call | solution.py:452
  184.7 4.1 %copy.17 = bf16[512,3584]{1,0:T(8,128)(2,1)} copy(bf16[512,3584]{1,0:T(8,128)(2,1)} %decoder.1) | data formatting | bytes 7340032

commit v6 on v5

--- a/solution.py
+++ b/solution.py
@@ -16,9 +16,9 @@
 HALF = 128
 TILE = 512
 SLOTS = 7
-KV_SLOTS = 7
+KV_SLOTS = 4
 X_SLOTS = 4
-KV_TOK = 16
+KV_TOK = 32
 
 
 def kernel(cfg, lens_ref, table_ref, gain_ref, x_in, wq, wk, wv, wo, wg, wu, wd, kc, vc, x_out,
@@ -260,6 +260,23 @@
         u = raws[2 * side + 1][...].astype(jnp.float32)
         u_s[:, pl.ds(pl.multiple_of(i * TILE, TILE), TILE)] = (g * (1.0 / (1.0 + jnp.exp(-g))) * u).astype(jnp.bfloat16)
 
+    def norm_rows(chunk, layer, i):
+        gains = gain_ref[...].astype(jnp.float32)
+        gain = gains[:1]
+        for other in range(1, layers):
+            gain = jnp.where(layer == other, gains[other:other + 1], gain)
+        src = pl.ds(pl.multiple_of(chunk * ROWS + i * 16, 16), 16)
+        dst = pl.ds(pl.multiple_of(i * 16, 16), 16)
+        parts = range(0, width, 256)
+        total = jnp.zeros((16, 256), jnp.float32)
+        for p in parts:
+            x = xs[src, p:p + 256].astype(jnp.float32)
+            total = total + x * x
+        inv = lax.rsqrt(jnp.sum(total, axis=-1, keepdims=True) / width + NORM_EPS)
+        for p in parts:
+            x = xs[src, p:p + 256].astype(jnp.float32)
+            a_s[dst, p:p + 256] = (x * inv * gain[:, p:p + 256]).astype(jnp.bfloat16)
+
     def stage(st, _):
         layer = lax.div(st, chunks)
         c = st - layer * chunks
@@ -267,67 +284,34 @@
         rows = pl.ds(pl.multiple_of(c * ROWS, ROWS), ROWS)
         w0 = st * n_w
 
-        @pl.when(st < chunks)
-        def _():
-            x_copy(c).wait()
-
-        @pl.when(st >= chunks)
-        def _():
-            new_wait(par)
-
-        gains = gain_ref[...].astype(jnp.float32)
-        gain = gains[:1]
-        for other in range(1, layers):
-            gain = jnp.where(layer == other, gains[other:other + 1], gain)
-
-        def norm_rows(i):
-            src = pl.ds(pl.multiple_of(c * ROWS + i * 16, 16), 16)
-            dst = pl.ds(pl.multiple_of(i * 16, 16), 16)
-            parts = range(0, width, 256)
-            total = jnp.zeros((16, 256), jnp.float32)
-            for p in parts:
-                x = xs[src, p:p + 256].astype(jnp.float32)
-                total = total + x * x
-            inv = lax.rsqrt(jnp.sum(total, axis=-1, keepdims=True) / width + NORM_EPS)
-            for p in parts:
-                x = xs[src, p:p + 256].astype(jnp.float32)
-                a_s[dst, p:p + 256] = (x * inv * gain[:, p:p + 256]).astype(jnp.bfloat16)
-
-        def norm(i, _):
-            norm_rows(2 * i)
-            norm_rows(2 * i + 1)
-            return 0
-
-        lax.fori_loop(0, ROWS // 32, norm, 0)
-
-        @pl.when(st >= 1)
-        def _():
-            for j in range(n_dn - 2, n_dn):
-                chip_sum(st - 1, j)
-
         slots = [w_wait(w0), w_wait(w0 + 1)]
         for i in range(2):
             raws[i][...] = dot(a_s[...], wbuf[slots[i]]).astype(jnp.bfloat16)
         w_next(w0)
         w_next(w0 + 1)
+
+        @pl.when(st >= 1)
+        def _():
+            for j in range(n_dn - 2, n_dn):
+                chip_sum(st - 1, j)
+
+        b0 = st * n_kv
         slots = [w_wait(w0 + 2), w_wait(w0 + 3)]
+        kv_copies(b0)[0].wait()
+        kv_copies(b0 + 1)[0].wait()
         raws[2][...] = dot(a_s[...], wbuf[slots[0]]).astype(jnp.bfloat16)
         rope(raws[0], q_s, 0, 1, rows)
         rope(raws[1], q_s, 2, 1, rows)
         v = dot(a_s[...], wbuf[slots[1]]).astype(jnp.bfloat16).astype(jnp.float32)
+        logits(0, st, 0)
         rope(raws[2], k_s, 0, 2, rows)
         for h in range(4):
             for j in range(2):
                 v_s[j, pl.ds(h, ROWS, 4)] = v[:, (h // 2) * 256 + j * 128:(h // 2) * 256 + j * 128 + 128]
             len4[pl.ds(h, ROWS, 4)] = len_s[rows]
-
-        b0 = st * n_kv
-        kv_copies(b0)[0].wait()
-        logits(0, st, 0)
-        k_next(b0)
-        kv_copies(b0 + 1)[0].wait()
         soft(0, c, 0)
         logits(1, st, 1)
+        k_next(b0)
         k_next(b0 + 1)
 
         def half(side, b):
@@ -351,16 +335,16 @@
 
         lax.fori_loop(0, n_kv // 2 - 1, block, 0)
         kv_copies(b0 + n_kv - 2)[1].wait()
+        kv_copies(b0 + n_kv - 1)[1].wait()
         mix(0, st, n_kv - 2)
         soft(1, c, n_kv - 1)
-        v_next(b0 + n_kv - 2)
-        kv_copies(b0 + n_kv - 1)[1].wait()
         mix(1, st, n_kv - 1)
-        v_next(b0 + n_kv - 1)
         for h in range(4):
             for j in range(2):
                 at = h * 256 + j * 128
                 att_s[:, at:at + 128] = q_s[j, pl.ds(h, ROWS, 4)].astype(jnp.bfloat16)
+        v_next(b0 + n_kv - 2)
+        v_next(b0 + n_kv - 1)
 
         def ff_tile(side, i):
             gt = w0 + n_q + 2 + 2 * i
@@ -385,7 +369,13 @@
         def _():
             finish(1 - par)
 
-        def down(j, _):
+        following = st + 1
+        turn = lax.rem(following, chunks)
+        source = turn + lax.div(following, stages) * (c - turn)
+        n_norm = 4
+        groups = ROWS // 16 // n_norm
+
+        def down(j, with_norm):
             gt = w0 + n_q + 2 + 2 * n_ff + j
             s0 = w_wait(gt)
 
@@ -398,6 +388,9 @@
                 chip_sum(st, j - 2)
 
             gj = st * n_dn + j
+            if with_norm:
+                for i in range(groups):
+                    norm_rows(source, lax.div(following, chunks), (j - (n_dn - n_norm)) * groups + i)
             ybuf[lax.rem(gj, X_SLOTS)] = dot(u_s[...], wbuf[s0]) + dot(att_s[...], wobuf[j])
             chip_copy(gj).start()
             w_next(gt)
@@ -406,11 +399,35 @@
             def _():
                 wo_copy(layer + 1, j).start()
 
+        def down_plain(j, _):
+            down(j, False)
             return 0
 
-        lax.fori_loop(0, n_dn, down, 0)
+        def down_norm(j, _):
+            down(j, True)
+            return 0
+
+        lax.fori_loop(0, n_dn - n_norm, down_plain, 0)
+
+        @pl.when(following < chunks)
+        def _():
+            x_copy(turn).wait()
+
+        @pl.when((following >= chunks) & (following < stages))
+        def _():
+            new_wait(turn)
+
+        lax.fori_loop(n_dn - n_norm, n_dn, down_norm, 0)
         return 0
 
+    x_copy(0).wait()
+
+    def first(i, _):
+        norm_rows(0, 0, 2 * i)
+        norm_rows(0, 0, 2 * i + 1)
+        return 0
+
+    lax.fori_loop(0, ROWS // 32, first, 0)
     for raw in raws:
         raw[...] = jnp.zeros_like(raw)
     lax.fori_loop(0, stages, stage, 0)

time: 189 us -> 182 us (0.963)
  Pallas kernels: 185 us -> 178 us
    pallas_call x1, Pallas kernels: 185 us -> 178 us  [per_device(): pl.pallas_call(functools.partial(kernel, (layers, tokens, width, seq, kv_...]
where the time goes in v6:
time: 182 us
  Pallas kernels  178 us (98%)
  local copies, waits for them, and re-layouts  4.11 us (2%)
    pallas_call x1, Pallas kernels, per_device(): pl.pallas_call(functools.partial(kernel, (layers, tokens, width, seq, kv_...  178 us
    unnamed x1, local copies, waits for them, and re-layouts  4.11 us

profile of v6, /device:TPU:0, one launch (start us, length us, event | category | flops | bytes accessed | tf_op | source)
XLA Modules:
  0.0 182.1 jit_solution(5295750459638671353)
XLA Ops:
  0.0 178.0 %decoder.1 = bf16[512,3584]{1,0:T(8,128)(2,1)} custom-call(s32[1,512]{1,0:T(1,128)} %bitcast.13, f32[32,384]{1,0:T(8,128)} %constant.2.clone.table_ref, bf16[2,3584]{1,0:T(2,128)(2,1)} %gain_ref.1, bf16[512,3584]{1,0:T(8,128)(2,1)} %x_in.1, bf16[2,3584,1024]{2,1,0:T(8,128)(2,1)} %wq.1, bf16[2,3584,512]{2,1,0:T(8,128)(2,1)} %wk.1, bf16[2,3584,512]{2,1,0:T(8,128)(2,1)} %wv.1, ...), custom_call_target="tpu_custom_call" | custom-call | tf_op jit(solution)/shard_map/decoder/pallas_call | solution.py:469
  178.0 4.1 %copy.17 = bf16[512,3584]{1,0:T(8,128)(2,1)} copy(bf16[512,3584]{1,0:T(8,128)(2,1)} %decoder.1) | data formatting | bytes 7340032

commit v7 on v6

--- a/solution.py
+++ b/solution.py
@@ -15,14 +15,14 @@
 ROWS = 256
 HALF = 128
 TILE = 512
-SLOTS = 7
-KV_SLOTS = 4
+SLOTS = 6
+KV_SLOTS = 5
 X_SLOTS = 4
 KV_TOK = 32
 
 
 def kernel(cfg, lens_ref, table_ref, gain_ref, x_in, wq, wk, wv, wo, wg, wu, wd, kc, vc, x_out,
-           xs, a_s, q_s, k_s, v_s, att_s, u_s, raws, cos_ref, sin_ref, len_s, len4, sidx, s_s, p_s, o_s, wbuf, wobuf, kbuf, vbuf, ybuf, irecv, rown, xrecv,
+           xs, a_s, q_s, k_s, v_s, att_s, u_s, raws, saved, cos_ref, sin_ref, len_s, len4, sidx, s_s, p_s, o_s, wbuf, wobuf, kbuf, vbuf, ybuf, irecv, rown, xrecv,
            wsem, wosem, kvsem, xsem, isend, irsem, xsend, xrsem, nsend, nrsem, osem):
     layers, tokens, width, seq, kv_heads = cfg
     tok_rows = seq * kv_heads * 2
@@ -33,7 +33,8 @@
     n_q = wq.shape[2] // TILE
     n_w = n_q + 2 + 2 * n_ff + n_dn
     n_kv = ROWS // KV_TOK
-    all_w, all_kv = stages * n_w, stages * n_kv
+    n_qkv = n_q + 2
+    all_w, all_kv = stages * n_w - n_qkv, stages * n_kv
 
     tp = lax.axis_index("tp")
     core = lax.rem(tp, 2)
@@ -43,8 +44,9 @@
     sib_row = pl.multiple_of((1 - core) * HALF, HALF)
 
     def w_start(gt):
-        st = lax.div(gt, n_w)
-        t = gt - st * n_w
+        t = gt + n_qkv * lax.div(lax.div(gt, n_w) + stages - 1, stages)
+        st = lax.div(t, n_w)
+        t = t - st * n_w
         layer = lax.div(st, chunks)
         slot = lax.rem(gt, SLOTS)
 
@@ -157,16 +159,15 @@
         rows = pl.ds(c * ROWS, ROWS)
         return pltpu.make_async_copy(xs.at[rows], x_out.at[rows], osem.at[c])
 
-    x_copy(0).start()
-    for g in range(SLOTS):
+    for c in range(chunks):
+        x_copy(c).start()
+    for g in range(n_qkv):
         w_start(jnp.int32(g))
     for g in range(KV_SLOTS):
         for cp in kv_copies(jnp.int32(g)):
             cp.start()
-    for j in range(n_dn):
-        wo_copy(0, j).start()
-    for c in range(1, chunks):
-        x_copy(c).start()
+    for g in range(n_qkv, SLOTS):
+        w_start(jnp.int32(g))
 
     barrier = pltpu.get_barrier_semaphore()
     for other in (sib, partner):
@@ -260,7 +261,7 @@
         u = raws[2 * side + 1][...].astype(jnp.float32)
         u_s[:, pl.ds(pl.multiple_of(i * TILE, TILE), TILE)] = (g * (1.0 / (1.0 + jnp.exp(-g))) * u).astype(jnp.bfloat16)
 
-    def norm_rows(chunk, layer, i):
+    def norm_rows(to, chunk, layer, i):
         gains = gain_ref[...].astype(jnp.float32)
         gain = gains[:1]
         for other in range(1, layers):
@@ -275,36 +276,65 @@
         inv = lax.rsqrt(jnp.sum(total, axis=-1, keepdims=True) / width + NORM_EPS)
         for p in parts:
             x = xs[src, p:p + 256].astype(jnp.float32)
-            a_s[dst, p:p + 256] = (x * inv * gain[:, p:p + 256]).astype(jnp.bfloat16)
+            to[dst, p:p + 256] = (x * inv * gain[:, p:p + 256]).astype(jnp.bfloat16)
 
     def stage(st, _):
         layer = lax.div(st, chunks)
         c = st - layer * chunks
         par = c
         rows = pl.ds(pl.multiple_of(c * ROWS, ROWS), ROWS)
-        w0 = st * n_w
-
-        slots = [w_wait(w0), w_wait(w0 + 1)]
-        for i in range(2):
-            raws[i][...] = dot(a_s[...], wbuf[slots[i]]).astype(jnp.bfloat16)
-        w_next(w0)
-        w_next(w0 + 1)
+        wf0 = st * n_w + n_qkv * (1 - lax.div(st + stages - 1, stages))
+        w0 = wf0 - n_qkv
+
+        def products(a, first, to):
+            for i in range(2):
+                to[first + i][...] = dot(a[...], wbuf[lax.rem(w0 + first + i, SLOTS)]).astype(jnp.bfloat16)
+
+        def rope_q():
+            rope(raws[0], q_s, 0, 1, rows)
+            rope(raws[1], q_s, 2, 1, rows)
+
+        @pl.when(st != 1)
+        def _():
+            for i in range(2):
+                w_wait(w0 + i)
+            products(a_s, 0, raws)
+
+            @pl.when(st == 0)
+            def _():
+                products(u_s, 0, saved)
+
+            w_next(w0)
+            w_next(w0 + 1)
 
         @pl.when(st >= 1)
         def _():
             for j in range(n_dn - 2, n_dn):
                 chip_sum(st - 1, j)
 
+        @pl.when(st != 1)
+        def _():
+            for i in range(2, 4):
+                w_wait(w0 + i)
+            rope_q()
+            products(a_s, 2, raws)
+
+            @pl.when(st == 0)
+            def _():
+                products(u_s, 2, saved)
+
+        @pl.when(st == 1)
+        def _():
+            for i in range(4):
+                raws[i][...] = saved[i][...]
+            rope_q()
+
         b0 = st * n_kv
-        slots = [w_wait(w0 + 2), w_wait(w0 + 3)]
         kv_copies(b0)[0].wait()
         kv_copies(b0 + 1)[0].wait()
-        raws[2][...] = dot(a_s[...], wbuf[slots[0]]).astype(jnp.bfloat16)
-        rope(raws[0], q_s, 0, 1, rows)
-        rope(raws[1], q_s, 2, 1, rows)
-        v = dot(a_s[...], wbuf[slots[1]]).astype(jnp.bfloat16).astype(jnp.float32)
         logits(0, st, 0)
         rope(raws[2], k_s, 0, 2, rows)
+        v = raws[3][...].astype(jnp.float32)
         for h in range(4):
             for j in range(2):
                 v_s[j, pl.ds(h, ROWS, 4)] = v[:, (h // 2) * 256 + j * 128:(h // 2) * 256 + j * 128 + 128]
@@ -324,13 +354,13 @@
             k_next(b0 + b + 1)
 
         def block(i, _):
-            half(1, 2 * i + 1)
-
-            @pl.when((i == 0) | (i == 2))
-            def _():
-                w_next(w0 + n_q + lax.div(i, 2))
-
-            half(0, 2 * i + 2)
+            for side, at in ((1, 1), (0, 2)):
+                half(side, 2 * i + at)
+
+                @pl.when((i == n_kv // 2 - 2) & (st != 1))
+                def _():
+                    w_next(w0 + n_q + at - 1)
+
             return 0
 
         lax.fori_loop(0, n_kv // 2 - 1, block, 0)
@@ -347,7 +377,7 @@
         v_next(b0 + n_kv - 1)
 
         def ff_tile(side, i):
-            gt = w0 + n_q + 2 + 2 * i
+            gt = wf0 + 2 * i
             s0, s1 = w_wait(gt), w_wait(gt + 1)
             swiglu(1 - side, lax.rem(i + n_ff - 1, n_ff))
             raws[2 * side][...] = dot(a_s[...], wbuf[s0]).astype(jnp.bfloat16)
@@ -355,6 +385,10 @@
             w_next(gt)
             w_next(gt + 1)
 
+            @pl.when(st == 0)
+            def _():
+                wo_copy(0, i).start()
+
         def ff(i, _):
             ff_tile(0, 2 * i)
             ff_tile(1, 2 * i + 1)
@@ -376,7 +410,7 @@
         groups = ROWS // 16 // n_norm
 
         def down(j, with_norm):
-            gt = w0 + n_q + 2 + 2 * n_ff + j
+            gt = wf0 + 2 * n_ff + j
             s0 = w_wait(gt)
 
             @pl.when(c == 0)
@@ -390,7 +424,7 @@
             gj = st * n_dn + j
             if with_norm:
                 for i in range(groups):
-                    norm_rows(source, lax.div(following, chunks), (j - (n_dn - n_norm)) * groups + i)
+                    norm_rows(a_s, source, lax.div(following, chunks), (j - (n_dn - n_norm)) * groups + i)
             ybuf[lax.rem(gj, X_SLOTS)] = dot(u_s[...], wbuf[s0]) + dot(att_s[...], wobuf[j])
             chip_copy(gj).start()
             w_next(gt)
@@ -409,10 +443,6 @@
 
         lax.fori_loop(0, n_dn - n_norm, down_plain, 0)
 
-        @pl.when(following < chunks)
-        def _():
-            x_copy(turn).wait()
-
         @pl.when((following >= chunks) & (following < stages))
         def _():
             new_wait(turn)
@@ -420,14 +450,15 @@
         lax.fori_loop(n_dn - n_norm, n_dn, down_norm, 0)
         return 0
 
-    x_copy(0).wait()
-
-    def first(i, _):
-        norm_rows(0, 0, 2 * i)
-        norm_rows(0, 0, 2 * i + 1)
-        return 0
-
-    lax.fori_loop(0, ROWS // 32, first, 0)
+    for c, to in enumerate((a_s, u_s)):
+        x_copy(c).wait()
+
+        def first(i, _):
+            norm_rows(to, c, 0, 2 * i)
+            norm_rows(to, c, 0, 2 * i + 1)
+            return 0
+
+        lax.fori_loop(0, ROWS // 32, first, 0)
     for raw in raws:
         raw[...] = jnp.zeros_like(raw)
     lax.fori_loop(0, stages, stage, 0)
@@ -479,6 +510,7 @@
                 pltpu.VMEM((2, 4 * ROWS, half), f32),
                 pltpu.VMEM((ROWS, w_q.shape[2]), bf),
                 pltpu.VMEM((ROWS, w_gate.shape[2]), bf),
+                [pltpu.VMEM((ROWS, TILE), bf)] * 4,
                 [pltpu.VMEM((ROWS, TILE), bf)] * 4,
                 pltpu.VMEM((tokens, half), f32),
                 pltpu.VMEM((tokens, half), f32),

time: 182 us -> 183 us (level)
  no operation moved by 1% of the time
where the time goes in v7:
time: 183 us
  Pallas kernels  179 us (98%)
  local copies, waits for them, and re-layouts  4.11 us (2%)
    pallas_call x1, Pallas kernels, per_device(): pl.pallas_call(functools.partial(kernel, (layers, tokens, width, seq, kv_...  179 us
    unnamed x1, local copies, waits for them, and re-layouts  4.11 us

profile of v7, /device:TPU:0, one launch (start us, length us, event | category | flops | bytes accessed | tf_op | source)
XLA Modules:
  0.0 183.2 jit_solution(14211399265082528248)
XLA Ops:
  0.0 179.1 %decoder.1 = bf16[512,3584]{1,0:T(8,128)(2,1)} custom-call(s32[1,512]{1,0:T(1,128)} %bitcast.13, f32[32,384]{1,0:T(8,128)} %constant.2.clone.table_ref, bf16[2,3584]{1,0:T(2,128)(2,1)} %gain_ref.1, bf16[512,3584]{1,0:T(8,128)(2,1)} %x_in.1, bf16[2,3584,1024]{2,1,0:T(8,128)(2,1)} %wq.1, bf16[2,3584,512]{2,1,0:T(8,128)(2,1)} %wk.1, bf16[2,3584,512]{2,1,0:T(8,128)(2,1)} %wv.1, ...), custom_call_target="tpu_custom_call" | custom-call | tf_op jit(solution)/shard_map/decoder/pallas_call | solution.py:500
  179.1 4.1 %copy.17 = bf16[512,3584]{1,0:T(8,128)(2,1)} copy(bf16[512,3584]{1,0:T(8,128)(2,1)} %decoder.1) | data formatting | bytes 7340032

commit v8 on v6

--- a/solution.py
+++ b/solution.py
@@ -346,23 +346,32 @@
         v_next(b0 + n_kv - 2)
         v_next(b0 + n_kv - 1)
 
-        def ff_tile(side, i):
+        def ff_dots(side, i):
             gt = w0 + n_q + 2 + 2 * i
-            s0, s1 = w_wait(gt), w_wait(gt + 1)
-            swiglu(1 - side, lax.rem(i + n_ff - 1, n_ff))
-            raws[2 * side][...] = dot(a_s[...], wbuf[s0]).astype(jnp.bfloat16)
-            raws[2 * side + 1][...] = dot(a_s[...], wbuf[s1]).astype(jnp.bfloat16)
+            raws[2 * side][...] = dot(a_s[...], wbuf[lax.rem(gt, SLOTS)]).astype(jnp.bfloat16)
+            raws[2 * side + 1][...] = dot(a_s[...], wbuf[lax.rem(gt + 1, SLOTS)]).astype(jnp.bfloat16)
+
+        def ff(i, _):
+            gt = w0 + n_q + 2 + 4 * i
+            for k in range(4):
+                w_wait(gt + k)
+            swiglu(1, lax.rem(2 * i + n_ff - 1, n_ff))
+            ff_dots(0, 2 * i)
+            swiglu(0, 2 * i)
+            ff_dots(1, 2 * i + 1)
+            for k in range(4):
+                w_next(gt + k)
+            return 0
+
+        lax.fori_loop(0, n_ff // 2, ff, 0)
+        if n_ff % 2:
+            gt = w0 + n_q + 2 + 2 * (n_ff - 1)
+            w_wait(gt)
+            w_wait(gt + 1)
+            swiglu(1, n_ff - 2)
+            ff_dots(0, n_ff - 1)
             w_next(gt)
             w_next(gt + 1)
-
-        def ff(i, _):
-            ff_tile(0, 2 * i)
-            ff_tile(1, 2 * i + 1)
-            return 0
-
-        lax.fori_loop(0, n_ff // 2, ff, 0)
-        if n_ff % 2:
-            ff_tile(0, n_ff - 1)
         swiglu((n_ff - 1) % 2, n_ff - 1)
 
         @pl.when(st >= 1)

time: 182 us -> 193 us (1.060)
  Pallas kernels: 178 us -> 189 us
    pallas_call x1, Pallas kernels: 178 us -> 189 us  [per_device(): pl.pallas_call(functools.partial(kernel, (layers, tokens, width, seq, kv_...]
where the time goes in v8:
time: 193 us
  Pallas kernels  189 us (98%)
  local copies, waits for them, and re-layouts  4.11 us (2%)
    pallas_call x1, Pallas kernels, per_device(): pl.pallas_call(functools.partial(kernel, (layers, tokens, width, seq, kv_...  189 us
    unnamed x1, local copies, waits for them, and re-layouts  4.11 us

profile of v8, /device:TPU:0, one launch (start us, length us, event | category | flops | bytes accessed | tf_op | source)
XLA Modules:
  0.0 193.2 jit_solution(4573073472048579222)
XLA Ops:
  0.0 189.1 %decoder.1 = bf16[512,3584]{1,0:T(8,128)(2,1)} custom-call(s32[1,512]{1,0:T(1,128)} %bitcast.13, f32[32,384]{1,0:T(8,128)} %constant.2.clone.table_ref, bf16[2,3584]{1,0:T(2,128)(2,1)} %gain_ref.1, bf16[512,3584]{1,0:T(8,128)(2,1)} %x_in.1, bf16[2,3584,1024]{2,1,0:T(8,128)(2,1)} %wq.1, bf16[2,3584,512]{2,1,0:T(8,128)(2,1)} %wk.1, bf16[2,3584,512]{2,1,0:T(8,128)(2,1)} %wv.1, ...), custom_call_target="tpu_custom_call" | custom-call | tf_op jit(solution)/shard_map/decoder/pallas_call | solution.py:478
  189.1 4.1 %copy.17 = bf16[512,3584]{1,0:T(8,128)(2,1)} copy(bf16[512,3584]{1,0:T(8,128)(2,1)} %decoder.1) | data formatting | bytes 7340032

commit v9 on v6

--- a/solution.py
+++ b/solution.py
@@ -15,8 +15,8 @@
 ROWS = 256
 HALF = 128
 TILE = 512
-SLOTS = 7
-KV_SLOTS = 4
+SLOTS = 6
+KV_SLOTS = 5
 X_SLOTS = 4
 KV_TOK = 32
 
@@ -158,13 +158,13 @@
         return pltpu.make_async_copy(xs.at[rows], x_out.at[rows], osem.at[c])
 
     x_copy(0).start()
-    for g in range(SLOTS):
+    for g in range(n_q + 2):
         w_start(jnp.int32(g))
     for g in range(KV_SLOTS):
         for cp in kv_copies(jnp.int32(g)):
             cp.start()
-    for j in range(n_dn):
-        wo_copy(0, j).start()
+    for g in range(n_q + 2, SLOTS):
+        w_start(jnp.int32(g))
     for c in range(1, chunks):
         x_copy(c).start()
 
@@ -324,13 +324,13 @@
             k_next(b0 + b + 1)
 
         def block(i, _):
-            half(1, 2 * i + 1)
-
-            @pl.when((i == 0) | (i == 2))
-            def _():
-                w_next(w0 + n_q + lax.div(i, 2))
-
-            half(0, 2 * i + 2)
+            for side, at in ((1, 1), (0, 2)):
+                half(side, 2 * i + at)
+
+                @pl.when(i == n_kv // 2 - 2)
+                def _():
+                    w_next(w0 + n_q + at - 1)
+
             return 0
 
         lax.fori_loop(0, n_kv // 2 - 1, block, 0)
@@ -354,6 +354,10 @@
             raws[2 * side + 1][...] = dot(a_s[...], wbuf[s1]).astype(jnp.bfloat16)
             w_next(gt)
             w_next(gt + 1)
+
+            @pl.when(st == 0)
+            def _():
+                wo_copy(0, i).start()
 
         def ff(i, _):
             ff_tile(0, 2 * i)

time: 182 us -> 175 us (0.962)
  Pallas kernels: 178 us -> 171 us
    pallas_call x1, Pallas kernels: 178 us -> 171 us  [per_device(): pl.pallas_call(functools.partial(kernel, (layers, tokens, width, seq, kv_...]
where the time goes in v9:
time: 175 us
  Pallas kernels  171 us (98%)
  local copies, waits for them, and re-layouts  4.11 us (2%)
    pallas_call x1, Pallas kernels, per_device(): pl.pallas_call(functools.partial(kernel, (layers, tokens, width, seq, kv_...  171 us
    unnamed x1, local copies, waits for them, and re-layouts  4.11 us

profile of v9, /device:TPU:0, one launch (start us, length us, event | category | flops | bytes accessed | tf_op | source)
XLA Modules:
  0.0 174.7 jit_solution(5037722937674834011)
XLA Ops:
  0.0 170.6 %decoder.1 = bf16[512,3584]{1,0:T(8,128)(2,1)} custom-call(s32[1,512]{1,0:T(1,128)} %bitcast.13, f32[32,384]{1,0:T(8,128)} %constant.2.clone.table_ref, bf16[2,3584]{1,0:T(2,128)(2,1)} %gain_ref.1, bf16[512,3584]{1,0:T(8,128)(2,1)} %x_in.1, bf16[2,3584,1024]{2,1,0:T(8,128)(2,1)} %wq.1, bf16[2,3584,512]{2,1,0:T(8,128)(2,1)} %wk.1, bf16[2,3584,512]{2,1,0:T(8,128)(2,1)} %wv.1, ...), custom_call_target="tpu_custom_call" | custom-call | tf_op jit(solution)/shard_map/decoder/pallas_call | solution.py:473
  170.6 4.1 %copy.17 = bf16[512,3584]{1,0:T(8,128)(2,1)} copy(bf16[512,3584]{1,0:T(8,128)(2,1)} %decoder.1) | data formatting | bytes 7340032
